TPU v7x, 32 devices: a 4x4x1 block of a 4x4x8 slice. The times are simulated.
32 devices in a mesh: dp: 1 (over z), cp: 32 (over y, x, core).
Axes of the slice: x: 4, y: 4, z: 1, core: 2. Of those that a mesh axis runs over, the one named last changes fastest.
The devices are a block of a 4x4x8 slice.
Arguments:
- query: bfloat16 [2, 1024, 32, 256], P('dp', 'cp')
- key: bfloat16 [2, 1024, 256], P('dp', 'cp')
- value: bfloat16 [2, 1024, 256], P('dp', 'cp')
- positions: int32 [1024], P(('dp', 'cp'))
- grad_out: bfloat16 [2, 1024, 32, 256], P('dp', 'cp')
Outputs:
- output 1: bfloat16 [2, 1024, 32, 256], P('dp', 'cp')
- output 2: bfloat16 [2, 1024, 32, 256], P('dp', 'cp')
- output 3: bfloat16 [2, 1024, 256], P('dp', 'cp')
- output 4: bfloat16 [2, 1024, 256], P('dp', 'cp')
All inputs are finite; a program needn't handle non-finite values.
Results may differ from a plain program's by a relative error of at most 0.00819063.
Values are sent between devices in bfloat16 or wider.
A program may use at most 768 MiB of HBM per device.

v0:
```python
import jax
import jax.numpy as jnp
from jax import lax
from jax.sharding import PartitionSpec as P

ROPE_BASE = 10000


def rope_tables(positions, head):
    half_dim = head // 2
    inv_freq = jnp.power(jnp.float32(ROPE_BASE), -2.0 * jnp.arange(half_dim, dtype=jnp.float32) / head)
    angles = positions.astype(jnp.float32)[..., None] * inv_freq
    angles = jnp.concatenate([angles, angles], axis=-1)
    return jnp.cos(angles), jnp.sin(angles)


def rotate(values, cos_tab, sin_tab):
    half_dim = values.shape[-1] // 2
    turned = jnp.concatenate([-values[..., half_dim:], values[..., :half_dim]], axis=-1)
    return values * cos_tab + turned * sin_tab


def solution(mesh):
    cp_size = mesh.shape['cp']
    shift_pairs = [(source, (source + 1) % cp_size) for source in range(cp_size)]
    query_spec = P('dp', 'cp', None, None)
    kv_spec = P('dp', 'cp', None)
    pos_spec = P(('dp', 'cp'))

    def per_device(query, key, value, positions, grad_out):
        batch, blk_len, heads, head = query.shape
        scale = head ** -0.5
        my_idx = lax.axis_index('cp')
        cos_tab, sin_tab = rope_tables(positions, head)
        cos_q = cos_tab[None, :, None, :]
        sin_q = sin_tab[None, :, None, :]
        query_rot = rotate(query, cos_q, sin_q).astype(jnp.bfloat16)
        key_rot = rotate(key, cos_tab[None], sin_tab[None]).astype(jnp.bfloat16)
        local_idx = jnp.arange(blk_len)
        diag_mask = (local_idx[None, :] <= local_idx[:, None])[None, :, None, :]

        def block_scores(key_blk, causal_mask):
            scores = jnp.einsum('crie,cle->cril', query_rot, key_blk, preferred_element_type=jnp.float32) * scale
            if causal_mask is None:
                return scores
            return jnp.where(causal_mask, scores, -jnp.inf)

        def forward_block(key_blk, value_blk, state, causal_mask):
            run_max, run_sum, out_acc = state
            scores = block_scores(key_blk, causal_mask)
            new_max = jnp.maximum(run_max, jnp.max(scores, axis=-1))
            factor = jnp.exp(run_max - new_max)
            weights = jnp.exp(scores - new_max[..., None])
            run_sum = run_sum * factor + jnp.sum(weights, axis=-1)
            out_acc = out_acc * factor[..., None] + jnp.einsum('cril,cle->crie', weights.astype(jnp.bfloat16), value_blk, preferred_element_type=jnp.float32)
            return new_max, run_sum, out_acc

        init_state = (jnp.full((batch, blk_len, heads), -jnp.inf, jnp.float32), jnp.zeros((batch, blk_len, heads), jnp.float32), jnp.zeros((batch, blk_len, heads, head), jnp.float32))
        state = forward_block(key_rot, value, init_state, diag_mask)

        def forward_step(step, carry):
            key_blk, value_blk, state_in = carry
            key_blk, value_blk = lax.ppermute((key_blk, value_blk), 'cp', shift_pairs)
            state_out = lax.cond(step <= my_idx, lambda prev: forward_block(key_blk, value_blk, prev, None), lambda prev: prev, state_in)
            return key_blk, value_blk, state_out

        fwd_carry = lax.fori_loop(1, cp_size, forward_step, (key_rot, value, state))
        run_max, run_sum, out_acc = fwd_carry[2]
        attn_out = (out_acc / run_sum[..., None]).astype(jnp.bfloat16)
        log_sum = run_max + jnp.log(run_sum)
        delta = jnp.einsum('bqhd,bqhd->bqh', grad_out, attn_out, preferred_element_type=jnp.float32)

        def backward_block(key_blk, value_blk, grads, causal_mask):
            dquery_acc, dkey_blk, dvalue_blk = grads
            scores = block_scores(key_blk, causal_mask)
            probs_f = jnp.exp(scores - log_sum[..., None])
            dprobs = jnp.einsum('crie,cle->cril', grad_out, value_blk, preferred_element_type=jnp.float32)
            dscore = (probs_f * (dprobs - delta[..., None])).astype(jnp.bfloat16)
            dquery_acc = dquery_acc + jnp.einsum('cril,cle->crie', dscore, key_blk, preferred_element_type=jnp.float32) * scale
            dkey_blk = dkey_blk + jnp.einsum('cril,crie->cle', dscore, query_rot, preferred_element_type=jnp.float32) * scale
            dvalue_blk = dvalue_blk + jnp.einsum('cril,crie->cle', probs_f.astype(jnp.bfloat16), grad_out, preferred_element_type=jnp.float32)
            return dquery_acc, dkey_blk, dvalue_blk

        zero_kv = jnp.zeros((batch, blk_len, head), jnp.float32)
        grads = backward_block(key_rot, value, (jnp.zeros((batch, blk_len, heads, head), jnp.float32), zero_kv, zero_kv), diag_mask)

        def backward_step(step, carry):
            key_blk, value_blk, dquery_acc, dkey_blk, dvalue_blk = carry
            key_blk, value_blk, dkey_blk, dvalue_blk = lax.ppermute((key_blk, value_blk, dkey_blk, dvalue_blk), 'cp', shift_pairs)
            grads_new = lax.cond(step <= my_idx, lambda prev: backward_block(key_blk, value_blk, prev, None), lambda prev: prev, (dquery_acc, dkey_blk, dvalue_blk))
            return (key_blk, value_blk) + tuple(grads_new)

        bwd_carry = lax.fori_loop(1, cp_size, backward_step, (key_rot, value) + tuple(grads))
        dkey_home, dvalue_home = lax.ppermute((bwd_carry[3], bwd_carry[4]), 'cp', shift_pairs)
        grad_query = rotate(bwd_carry[2], cos_q, -sin_q).astype(jnp.bfloat16)
        grad_key = rotate(dkey_home, cos_tab[None], -sin_tab[None]).astype(jnp.bfloat16)
        return attn_out, grad_query, grad_key, dvalue_home.astype(jnp.bfloat16)

    return jax.shard_map(per_device, mesh=mesh, in_specs=(query_spec, kv_spec, kv_spec, pos_spec, query_spec), out_specs=(query_spec, query_spec, kv_spec, kv_spec), check_vma=False)
```

profile of v0, /device:TPU:97, one launch (start us, length us, event | category | flops | bytes accessed | tf_op | source)
XLA Modules:
  0.0 667.6 jit_solution(13101888978899817143)
XLA Ops:
  6.8 220.3 %while.42 = (s32[]{:T(128)}, bf16[2,32,256]{2,1,0:T(8,128)(2,1)S(1)}, bf16[2,32,256]{2,1,0:T(8,128)(2,1)S(1)}, f32[2,32,32]{2,1,0:T(8,128)S(1)}, f32[2,32,32]{2,...) while((s32[]{:T(128)}, ...), condition=%wide.region_7.8_spmd, body=%wide.region_2.7_spmd.sunk | while | flops 68554752 | bytes 6619427 | solution.py:67
  32.7 6.7 %collective-permute-done = bf16[2,32,256]{2,1,0:T(8,128)(2,1)S(1)} collective-permute-done((bf16[2,32,256]{2,1,0:T(8,128)(2,1)S(1)}, bf16[2,32,256]{2,1,0:T(8,128)(2,1)S(1)}, u32[]{:S(2)}, u32[]{:S(2)}) %collective-permute-start) | collective-permute-done | bytes 32800 | tf_op jit(solution)/shard_map/while/body/eval_jaxpr/ppermute | solution.py:63
  39.8 6.7 %collective-permute-done = bf16[2,32,256]{2,1,0:T(8,128)(2,1)S(1)} collective-permute-done((bf16[2,32,256]{2,1,0:T(8,128)(2,1)S(1)}, bf16[2,32,256]{2,1,0:T(8,128)(2,1)S(1)}, u32[]{:S(2)}, u32[]{:S(2)}) %collective-permute-start) | collective-permute-done | bytes 32800 | tf_op jit(solution)/shard_map/while/body/eval_jaxpr/ppermute | solution.py:63
  54.0 6.7 %collective-permute-done = bf16[2,32,256]{2,1,0:T(8,128)(2,1)S(1)} collective-permute-done((bf16[2,32,256]{2,1,0:T(8,128)(2,1)S(1)}, bf16[2,32,256]{2,1,0:T(8,128)(2,1)S(1)}, u32[]{:S(2)}, u32[]{:S(2)}) %collective-permute-start) | collective-permute-done | bytes 32800 | tf_op jit(solution)/shard_map/while/body/eval_jaxpr/ppermute | solution.py:63
  96.8 6.7 %collective-permute-done = bf16[2,32,256]{2,1,0:T(8,128)(2,1)S(1)} collective-permute-done((bf16[2,32,256]{2,1,0:T(8,128)(2,1)S(1)}, bf16[2,32,256]{2,1,0:T(8,128)(2,1)S(1)}, u32[]{:S(2)}, u32[]{:S(2)}) %collective-permute-start) | collective-permute-done | bytes 32800 | tf_op jit(solution)/shard_map/while/body/eval_jaxpr/ppermute | solution.py:63
  103.9 6.7 %collective-permute-done = bf16[2,32,256]{2,1,0:T(8,128)(2,1)S(1)} collective-permute-done((bf16[2,32,256]{2,1,0:T(8,128)(2,1)S(1)}, bf16[2,32,256]{2,1,0:T(8,128)(2,1)S(1)}, u32[]{:S(2)}, u32[]{:S(2)}) %collective-permute-start) | collective-permute-done | bytes 32800 | tf_op jit(solution)/shard_map/while/body/eval_jaxpr/ppermute | solution.py:63
  111.1 6.7 %collective-permute-done = bf16[2,32,256]{2,1,0:T(8,128)(2,1)S(1)} collective-permute-done((bf16[2,32,256]{2,1,0:T(8,128)(2,1)S(1)}, bf16[2,32,256]{2,1,0:T(8,128)(2,1)S(1)}, u32[]{:S(2)}, u32[]{:S(2)}) %collective-permute-start) | collective-permute-done | bytes 32800 | tf_op jit(solution)/shard_map/while/body/eval_jaxpr/ppermute | solution.py:63
  118.2 6.7 %collective-permute-done = bf16[2,32,256]{2,1,0:T(8,128)(2,1)S(1)} collective-permute-done((bf16[2,32,256]{2,1,0:T(8,128)(2,1)S(1)}, bf16[2,32,256]{2,1,0:T(8,128)(2,1)S(1)}, u32[]{:S(2)}, u32[]{:S(2)}) %collective-permute-start) | collective-permute-done | bytes 32800 | tf_op jit(solution)/shard_map/while/body/eval_jaxpr/ppermute | solution.py:63
  125.3 6.7 %collective-permute-done = bf16[2,32,256]{2,1,0:T(8,128)(2,1)S(1)} collective-permute-done((bf16[2,32,256]{2,1,0:T(8,128)(2,1)S(1)}, bf16[2,32,256]{2,1,0:T(8,128)(2,1)S(1)}, u32[]{:S(2)}, u32[]{:S(2)}) %collective-permute-start) | collective-permute-done | bytes 32800 | tf_op jit(solution)/shard_map/while/body/eval_jaxpr/ppermute | solution.py:63
  132.4 6.7 %collective-permute-done = bf16[2,32,256]{2,1,0:T(8,128)(2,1)S(1)} collective-permute-done((bf16[2,32,256]{2,1,0:T(8,128)(2,1)S(1)}, bf16[2,32,256]{2,1,0:T(8,128)(2,1)S(1)}, u32[]{:S(2)}, u32[]{:S(2)}) %collective-permute-start) | collective-permute-done | bytes 32800 | tf_op jit(solution)/shard_map/while/body/eval_jaxpr/ppermute | solution.py:63
  139.6 6.7 %collective-permute-done = bf16[2,32,256]{2,1,0:T(8,128)(2,1)S(1)} collective-permute-done((bf16[2,32,256]{2,1,0:T(8,128)(2,1)S(1)}, bf16[2,32,256]{2,1,0:T(8,128)(2,1)S(1)}, u32[]{:S(2)}, u32[]{:S(2)}) %collective-permute-start) | collective-permute-done | bytes 32800 | tf_op jit(solution)/shard_map/while/body/eval_jaxpr/ppermute | solution.py:63
  146.7 6.7 %collective-permute-done = bf16[2,32,256]{2,1,0:T(8,128)(2,1)S(1)} collective-permute-done((bf16[2,32,256]{2,1,0:T(8,128)(2,1)S(1)}, bf16[2,32,256]{2,1,0:T(8,128)(2,1)S(1)}, u32[]{:S(2)}, u32[]{:S(2)}) %collective-permute-start) | collective-permute-done | bytes 32800 | tf_op jit(solution)/shard_map/while/body/eval_jaxpr/ppermute | solution.py:63
  153.8 6.7 %collective-permute-done = bf16[2,32,256]{2,1,0:T(8,128)(2,1)S(1)} collective-permute-done((bf16[2,32,256]{2,1,0:T(8,128)(2,1)S(1)}, bf16[2,32,256]{2,1,0:T(8,128)(2,1)S(1)}, u32[]{:S(2)}, u32[]{:S(2)}) %collective-permute-start) | collective-permute-done | bytes 32800 | tf_op jit(solution)/shard_map/while/body/eval_jaxpr/ppermute | solution.py:63
  161.0 6.7 %collective-permute-done = bf16[2,32,256]{2,1,0:T(8,128)(2,1)S(1)} collective-permute-done((bf16[2,32,256]{2,1,0:T(8,128)(2,1)S(1)}, bf16[2,32,256]{2,1,0:T(8,128)(2,1)S(1)}, u32[]{:S(2)}, u32[]{:S(2)}) %collective-permute-start) | collective-permute-done | bytes 32800 | tf_op jit(solution)/shard_map/while/body/eval_jaxpr/ppermute | solution.py:63
  168.1 6.7 %collective-permute-done = bf16[2,32,256]{2,1,0:T(8,128)(2,1)S(1)} collective-permute-done((bf16[2,32,256]{2,1,0:T(8,128)(2,1)S(1)}, bf16[2,32,256]{2,1,0:T(8,128)(2,1)S(1)}, u32[]{:S(2)}, u32[]{:S(2)}) %collective-permute-start) | collective-permute-done | bytes 32800 | tf_op jit(solution)/shard_map/while/body/eval_jaxpr/ppermute | solution.py:63
  175.2 6.7 %collective-permute-done = bf16[2,32,256]{2,1,0:T(8,128)(2,1)S(1)} collective-permute-done((bf16[2,32,256]{2,1,0:T(8,128)(2,1)S(1)}, bf16[2,32,256]{2,1,0:T(8,128)(2,1)S(1)}, u32[]{:S(2)}, u32[]{:S(2)}) %collective-permute-start) | collective-permute-done | bytes 32800 | tf_op jit(solution)/shard_map/while/body/eval_jaxpr/ppermute | solution.py:63
  182.3 6.7 %collective-permute-done = bf16[2,32,256]{2,1,0:T(8,128)(2,1)S(1)} collective-permute-done((bf16[2,32,256]{2,1,0:T(8,128)(2,1)S(1)}, bf16[2,32,256]{2,1,0:T(8,128)(2,1)S(1)}, u32[]{:S(2)}, u32[]{:S(2)}) %collective-permute-start) | collective-permute-done | bytes 32800 | tf_op jit(solution)/shard_map/while/body/eval_jaxpr/ppermute | solution.py:63
  203.7 6.8 %collective-permute-done = bf16[2,32,256]{2,1,0:T(8,128)(2,1)S(1)} collective-permute-done((bf16[2,32,256]{2,1,0:T(8,128)(2,1)S(1)}, bf16[2,32,256]{2,1,0:T(8,128)(2,1)S(1)}, u32[]{:S(2)}, u32[]{:S(2)}) %collective-permute-start) | collective-permute-done | bytes 32800 | tf_op jit(solution)/shard_map/while/body/eval_jaxpr/ppermute | solution.py:63
  210.9 7.8 %collective-permute-done = bf16[2,32,256]{2,1,0:T(8,128)(2,1)S(1)} collective-permute-done((bf16[2,32,256]{2,1,0:T(8,128)(2,1)S(1)}, bf16[2,32,256]{2,1,0:T(8,128)(2,1)S(1)}, u32[]{:S(2)}, u32[]{:S(2)}) %collective-permute-start) | collective-permute-done | bytes 32800 | tf_op jit(solution)/shard_map/while/body/eval_jaxpr/ppermute | solution.py:63
  219.1 7.8 %collective-permute-done = bf16[2,32,256]{2,1,0:T(8,128)(2,1)S(1)} collective-permute-done((bf16[2,32,256]{2,1,0:T(8,128)(2,1)S(1)}, bf16[2,32,256]{2,1,0:T(8,128)(2,1)S(1)}, u32[]{:S(2)}, u32[]{:S(2)}) %collective-permute-start) | collective-permute-done | bytes 32800 | tf_op jit(solution)/shard_map/while/body/eval_jaxpr/ppermute | solution.py:63
  235.9 416.7 %while.43 = (s32[]{:T(128)}, bf16[2,32,256]{2,1,0:T(8,128)(2,1)S(1)}, bf16[2,32,256]{2,1,0:T(8,128)(2,1)S(1)}, f32[2,32,32,256]{3,2,1,0:T(8,128)S(1)}, f32[2,32,...) while((s32[]{:T(128)}, ...), condition=%wide.region_11.12_spmd, body=%wide.region_8.11_spmd.sunk | while | flops 169263104 | bytes 15319487 | solution.py:93
  236.4 7.8 %collective-permute-done.3 = bf16[2,32,256]{2,1,0:T(8,128)(2,1)S(1)} collective-permute-done((bf16[2,32,256]{2,1,0:T(8,128)(2,1)S(1)}, bf16[2,32,256]{2,1,0:T(8,128)(2,1)S(1)}, u32[]{:S(2)}, u32[]{:S(2)}) %collective-permute-start.3) | collective-permute-done | bytes 32800 | tf_op jit(solution)/shard_map/while/body/eval_jaxpr/ppermute | solution.py:89
  256.2 7.6 %collective-permute-start.4 = (f32[2,32,256]{2,1,0:T(8,128)}, f32[2,32,256]{2,1,0:T(8,128)S(1)}, u32[]{:S(2)}, u32[]{:S(2)}) collective-permute-start(f32[2,32,256]{2,1,0:T(8,128)} %get-tuple-element.665), channel_id=1, source_target_pairs={{0,1},{1,2},{2,3},{3,4},{4,5},{5,6},{6,7},{7,8},{8,9},{9,10},{10,1... | collective-permute-start | bytes 196616 | tf_op jit(solution)/shard_map/while/body/eval_jaxpr/ppermute | solution.py:89
  287.7 10.2 %collective-permute-start.3 = (bf16[2,32,256]{2,1,0:T(8,128)(2,1)S(1)}, bf16[2,32,256]{2,1,0:T(8,128)(2,1)S(1)}, u32[]{:S(2)}, u32[]{:S(2)}) collective-permute-start(bf16[2,32,256]{2,1,0:T(8,128)(2,1)S(1)} %get-tuple-element.663), channel_id=1, source_target_pairs={{0,1},{1,2},{2,3},{3,4},{4,5},{5,6},{6,7},{7,8},{8,9},{9,10},{10,1... | collective-permute-start | bytes 98312 | tf_op jit(solution)/shard_map/while/body/eval_jaxpr/ppermute | solution.py:89
  328.2 8.1 %collective-permute-start.4 = (f32[2,32,256]{2,1,0:T(8,128)}, f32[2,32,256]{2,1,0:T(8,128)S(1)}, u32[]{:S(2)}, u32[]{:S(2)}) collective-permute-start(f32[2,32,256]{2,1,0:T(8,128)} %get-tuple-element.665), channel_id=1, source_target_pairs={{0,1},{1,2},{2,3},{3,4},{4,5},{5,6},{6,7},{7,8},{8,9},{9,10},{10,1... | collective-permute-start | bytes 196616 | tf_op jit(solution)/shard_map/while/body/eval_jaxpr/ppermute | solution.py:89
  360.9 9.0 %collective-permute-start.3 = (bf16[2,32,256]{2,1,0:T(8,128)(2,1)S(1)}, bf16[2,32,256]{2,1,0:T(8,128)(2,1)S(1)}, u32[]{:S(2)}, u32[]{:S(2)}) collective-permute-start(bf16[2,32,256]{2,1,0:T(8,128)(2,1)S(1)} %get-tuple-element.663), channel_id=1, source_target_pairs={{0,1},{1,2},{2,3},{3,4},{4,5},{5,6},{6,7},{7,8},{8,9},{9,10},{10,1... | collective-permute-start | bytes 98312 | tf_op jit(solution)/shard_map/while/body/eval_jaxpr/ppermute | solution.py:89
  427.0 7.4 %collective-permute-start.3 = (bf16[2,32,256]{2,1,0:T(8,128)(2,1)S(1)}, bf16[2,32,256]{2,1,0:T(8,128)(2,1)S(1)}, u32[]{:S(2)}, u32[]{:S(2)}) collective-permute-start(bf16[2,32,256]{2,1,0:T(8,128)(2,1)S(1)} %get-tuple-element.663), channel_id=1, source_target_pairs={{0,1},{1,2},{2,3},{3,4},{4,5},{5,6},{6,7},{7,8},{8,9},{9,10},{10,1... | collective-permute-start | bytes 98312 | tf_op jit(solution)/shard_map/while/body/eval_jaxpr/ppermute | solution.py:89
  491.8 8.6 %collective-permute-start.3 = (bf16[2,32,256]{2,1,0:T(8,128)(2,1)S(1)}, bf16[2,32,256]{2,1,0:T(8,128)(2,1)S(1)}, u32[]{:S(2)}, u32[]{:S(2)}) collective-permute-start(bf16[2,32,256]{2,1,0:T(8,128)(2,1)S(1)} %get-tuple-element.663), channel_id=1, source_target_pairs={{0,1},{1,2},{2,3},{3,4},{4,5},{5,6},{6,7},{7,8},{8,9},{9,10},{10,1... | collective-permute-start | bytes 98312 | tf_op jit(solution)/shard_map/while/body/eval_jaxpr/ppermute | solution.py:89
  557.9 7.1 %collective-permute-start.3 = (bf16[2,32,256]{2,1,0:T(8,128)(2,1)S(1)}, bf16[2,32,256]{2,1,0:T(8,128)(2,1)S(1)}, u32[]{:S(2)}, u32[]{:S(2)}) collective-permute-start(bf16[2,32,256]{2,1,0:T(8,128)(2,1)S(1)} %get-tuple-element.663), channel_id=1, source_target_pairs={{0,1},{1,2},{2,3},{3,4},{4,5},{5,6},{6,7},{7,8},{8,9},{9,10},{10,1... | collective-permute-start | bytes 98312 | tf_op jit(solution)/shard_map/while/body/eval_jaxpr/ppermute | solution.py:89
  623.8 7.3 %collective-permute-start.3 = (bf16[2,32,256]{2,1,0:T(8,128)(2,1)S(1)}, bf16[2,32,256]{2,1,0:T(8,128)(2,1)S(1)}, u32[]{:S(2)}, u32[]{:S(2)}) collective-permute-start(bf16[2,32,256]{2,1,0:T(8,128)(2,1)S(1)} %get-tuple-element.663), channel_id=1, source_target_pairs={{0,1},{1,2},{2,3},{3,4},{4,5},{5,6},{6,7},{7,8},{8,9},{9,10},{10,1... | collective-permute-start | bytes 98312 | tf_op jit(solution)/shard_map/while/body/eval_jaxpr/ppermute | solution.py:89
  641.9 9.3 %collective-permute-done.3 = bf16[2,32,256]{2,1,0:T(8,128)(2,1)S(1)} collective-permute-done((bf16[2,32,256]{2,1,0:T(8,128)(2,1)S(1)}, bf16[2,32,256]{2,1,0:T(8,128)(2,1)S(1)}, u32[]{:S(2)}, u32[]{:S(2)}) %collective-permute-start.3) | collective-permute-done | bytes 32800 | tf_op jit(solution)/shard_map/while/body/eval_jaxpr/ppermute | solution.py:89
  655.2 11.1 %collective-permute-done.7 = bf16[2,32,256]{2,1,0:T(8,128)(2,1)S(1)} collective-permute-done((bf16[2,32,256]{2,1,0:T(8,128)(2,1)S(1)}, bf16[2,32,256]{2,1,0:T(8,128)(2,1)S(1)}, u32[]{:S(2)}, u32[]{:S(2)}) %collective-permute-start.7) | collective-permute-done | bytes 32800 | tf_op jit(solution)/shard_map/ppermute | solution.py:94
  (652 shorter events, 448.9 us)
Async XLA Ops:
  267.7 13.9 %collective-permute-start.4 = (f32[2,32,256]{2,1,0:T(8,128)}, f32[2,32,256]{2,1,0:T(8,128)S(1)}, u32[]{:S(2)}, u32[]{:S(2)}) collective-permute-start(f32[2,32,256]{2,1,0:T(8,128)} %get-tuple-element.665), channel_id=1, source_target_pairs={{0,1},{1,2},{2,3},{3,4},{4,5},{5,6},{6,7},{7,8},{8,9},{9,10},{10,1... | collective-permute-start | bytes 196616 | tf_op jit(solution)/shard_map/while/body/eval_jaxpr/ppermute | solution.py:89
  282.9 16.5 %collective-permute-start.4 = (f32[2,32,256]{2,1,0:T(8,128)}, f32[2,32,256]{2,1,0:T(8,128)S(1)}, u32[]{:S(2)}, u32[]{:S(2)}) collective-permute-start(f32[2,32,256]{2,1,0:T(8,128)} %get-tuple-element.665), channel_id=1, source_target_pairs={{0,1},{1,2},{2,3},{3,4},{4,5},{5,6},{6,7},{7,8},{8,9},{9,10},{10,1... | collective-permute-start | bytes 196616 | tf_op jit(solution)/shard_map/while/body/eval_jaxpr/ppermute | solution.py:89
  286.2 13.2 %collective-permute-start.5 = (f32[2,32,256]{2,1,0:T(8,128)}, f32[2,32,256]{2,1,0:T(8,128)S(1)}, u32[]{:S(2)}, u32[]{:S(2)}) collective-permute-start(f32[2,32,256]{2,1,0:T(8,128)} %get-tuple-element.666), channel_id=1, source_target_pairs={{0,1},{1,2},{2,3},{3,4},{4,5},{5,6},{6,7},{7,8},{8,9},{9,10},{10,1... | collective-permute-start | bytes 196616 | tf_op jit(solution)/shard_map/while/body/eval_jaxpr/ppermute | solution.py:89
  300.7 16.5 %collective-permute-start.4 = (f32[2,32,256]{2,1,0:T(8,128)}, f32[2,32,256]{2,1,0:T(8,128)S(1)}, u32[]{:S(2)}, u32[]{:S(2)}) collective-permute-start(f32[2,32,256]{2,1,0:T(8,128)} %get-tuple-element.665), channel_id=1, source_target_pairs={{0,1},{1,2},{2,3},{3,4},{4,5},{5,6},{6,7},{7,8},{8,9},{9,10},{10,1... | collective-permute-start | bytes 196616 | tf_op jit(solution)/shard_map/while/body/eval_jaxpr/ppermute | solution.py:89
  304.2 13.0 %collective-permute-start.5 = (f32[2,32,256]{2,1,0:T(8,128)}, f32[2,32,256]{2,1,0:T(8,128)S(1)}, u32[]{:S(2)}, u32[]{:S(2)}) collective-permute-start(f32[2,32,256]{2,1,0:T(8,128)} %get-tuple-element.666), channel_id=1, source_target_pairs={{0,1},{1,2},{2,3},{3,4},{4,5},{5,6},{6,7},{7,8},{8,9},{9,10},{10,1... | collective-permute-start | bytes 196616 | tf_op jit(solution)/shard_map/while/body/eval_jaxpr/ppermute | solution.py:89
  328.2 14.4 %collective-permute-start.4 = (f32[2,32,256]{2,1,0:T(8,128)}, f32[2,32,256]{2,1,0:T(8,128)S(1)}, u32[]{:S(2)}, u32[]{:S(2)}) collective-permute-start(f32[2,32,256]{2,1,0:T(8,128)} %get-tuple-element.665), channel_id=1, source_target_pairs={{0,1},{1,2},{2,3},{3,4},{4,5},{5,6},{6,7},{7,8},{8,9},{9,10},{10,1... | collective-permute-start | bytes 196616 | tf_op jit(solution)/shard_map/while/body/eval_jaxpr/ppermute | solution.py:89
  343.8 13.1 %collective-permute-start.4 = (f32[2,32,256]{2,1,0:T(8,128)}, f32[2,32,256]{2,1,0:T(8,128)S(1)}, u32[]{:S(2)}, u32[]{:S(2)}) collective-permute-start(f32[2,32,256]{2,1,0:T(8,128)} %get-tuple-element.665), channel_id=1, source_target_pairs={{0,1},{1,2},{2,3},{3,4},{4,5},{5,6},{6,7},{7,8},{8,9},{9,10},{10,1... | collective-permute-start | bytes 196616 | tf_op jit(solution)/shard_map/while/body/eval_jaxpr/ppermute | solution.py:89
  358.2 13.1 %collective-permute-start.4 = (f32[2,32,256]{2,1,0:T(8,128)}, f32[2,32,256]{2,1,0:T(8,128)S(1)}, u32[]{:S(2)}, u32[]{:S(2)}) collective-permute-start(f32[2,32,256]{2,1,0:T(8,128)} %get-tuple-element.665), channel_id=1, source_target_pairs={{0,1},{1,2},{2,3},{3,4},{4,5},{5,6},{6,7},{7,8},{8,9},{9,10},{10,1... | collective-permute-start | bytes 196616 | tf_op jit(solution)/shard_map/while/body/eval_jaxpr/ppermute | solution.py:89
  372.6 11.9 %collective-permute-start.4 = (f32[2,32,256]{2,1,0:T(8,128)}, f32[2,32,256]{2,1,0:T(8,128)S(1)}, u32[]{:S(2)}, u32[]{:S(2)}) collective-permute-start(f32[2,32,256]{2,1,0:T(8,128)} %get-tuple-element.665), channel_id=1, source_target_pairs={{0,1},{1,2},{2,3},{3,4},{4,5},{5,6},{6,7},{7,8},{8,9},{9,10},{10,1... | collective-permute-start | bytes 196616 | tf_op jit(solution)/shard_map/while/body/eval_jaxpr/ppermute | solution.py:89
  395.5 13.1 %collective-permute-start.4 = (f32[2,32,256]{2,1,0:T(8,128)}, f32[2,32,256]{2,1,0:T(8,128)S(1)}, u32[]{:S(2)}, u32[]{:S(2)}) collective-permute-start(f32[2,32,256]{2,1,0:T(8,128)} %get-tuple-element.665), channel_id=1, source_target_pairs={{0,1},{1,2},{2,3},{3,4},{4,5},{5,6},{6,7},{7,8},{8,9},{9,10},{10,1... | collective-permute-start | bytes 196616 | tf_op jit(solution)/shard_map/while/body/eval_jaxpr/ppermute | solution.py:89
  409.9 13.1 %collective-permute-start.4 = (f32[2,32,256]{2,1,0:T(8,128)}, f32[2,32,256]{2,1,0:T(8,128)S(1)}, u32[]{:S(2)}, u32[]{:S(2)}) collective-permute-start(f32[2,32,256]{2,1,0:T(8,128)} %get-tuple-element.665), channel_id=1, source_target_pairs={{0,1},{1,2},{2,3},{3,4},{4,5},{5,6},{6,7},{7,8},{8,9},{9,10},{10,1... | collective-permute-start | bytes 196616 | tf_op jit(solution)/shard_map/while/body/eval_jaxpr/ppermute | solution.py:89
  424.3 11.9 %collective-permute-start.4 = (f32[2,32,256]{2,1,0:T(8,128)}, f32[2,32,256]{2,1,0:T(8,128)S(1)}, u32[]{:S(2)}, u32[]{:S(2)}) collective-permute-start(f32[2,32,256]{2,1,0:T(8,128)} %get-tuple-element.665), channel_id=1, source_target_pairs={{0,1},{1,2},{2,3},{3,4},{4,5},{5,6},{6,7},{7,8},{8,9},{9,10},{10,1... | collective-permute-start | bytes 196616 | tf_op jit(solution)/shard_map/while/body/eval_jaxpr/ppermute | solution.py:89
  437.5 13.1 %collective-permute-start.4 = (f32[2,32,256]{2,1,0:T(8,128)}, f32[2,32,256]{2,1,0:T(8,128)S(1)}, u32[]{:S(2)}, u32[]{:S(2)}) collective-permute-start(f32[2,32,256]{2,1,0:T(8,128)} %get-tuple-element.665), channel_id=1, source_target_pairs={{0,1},{1,2},{2,3},{3,4},{4,5},{5,6},{6,7},{7,8},{8,9},{9,10},{10,1... | collective-permute-start | bytes 196616 | tf_op jit(solution)/shard_map/while/body/eval_jaxpr/ppermute | solution.py:89
  461.6 13.1 %collective-permute-start.4 = (f32[2,32,256]{2,1,0:T(8,128)}, f32[2,32,256]{2,1,0:T(8,128)S(1)}, u32[]{:S(2)}, u32[]{:S(2)}) collective-permute-start(f32[2,32,256]{2,1,0:T(8,128)} %get-tuple-element.665), channel_id=1, source_target_pairs={{0,1},{1,2},{2,3},{3,4},{4,5},{5,6},{6,7},{7,8},{8,9},{9,10},{10,1... | collective-permute-start | bytes 196616 | tf_op jit(solution)/shard_map/while/body/eval_jaxpr/ppermute | solution.py:89
  476.0 11.9 %collective-permute-start.4 = (f32[2,32,256]{2,1,0:T(8,128)}, f32[2,32,256]{2,1,0:T(8,128)S(1)}, u32[]{:S(2)}, u32[]{:S(2)}) collective-permute-start(f32[2,32,256]{2,1,0:T(8,128)} %get-tuple-element.665), channel_id=1, source_target_pairs={{0,1},{1,2},{2,3},{3,4},{4,5},{5,6},{6,7},{7,8},{8,9},{9,10},{10,1... | collective-permute-start | bytes 196616 | tf_op jit(solution)/shard_map/while/body/eval_jaxpr/ppermute | solution.py:89
  489.2 13.1 %collective-permute-start.4 = (f32[2,32,256]{2,1,0:T(8,128)}, f32[2,32,256]{2,1,0:T(8,128)S(1)}, u32[]{:S(2)}, u32[]{:S(2)}) collective-permute-start(f32[2,32,256]{2,1,0:T(8,128)} %get-tuple-element.665), channel_id=1, source_target_pairs={{0,1},{1,2},{2,3},{3,4},{4,5},{5,6},{6,7},{7,8},{8,9},{9,10},{10,1... | collective-permute-start | bytes 196616 | tf_op jit(solution)/shard_map/while/body/eval_jaxpr/ppermute | solution.py:89
  503.6 11.9 %collective-permute-start.4 = (f32[2,32,256]{2,1,0:T(8,128)}, f32[2,32,256]{2,1,0:T(8,128)S(1)}, u32[]{:S(2)}, u32[]{:S(2)}) collective-permute-start(f32[2,32,256]{2,1,0:T(8,128)} %get-tuple-element.665), channel_id=1, source_target_pairs={{0,1},{1,2},{2,3},{3,4},{4,5},{5,6},{6,7},{7,8},{8,9},{9,10},{10,1... | collective-permute-start | bytes 196616 | tf_op jit(solution)/shard_map/while/body/eval_jaxpr/ppermute | solution.py:89
  526.4 13.1 %collective-permute-start.4 = (f32[2,32,256]{2,1,0:T(8,128)}, f32[2,32,256]{2,1,0:T(8,128)S(1)}, u32[]{:S(2)}, u32[]{:S(2)}) collective-permute-start(f32[2,32,256]{2,1,0:T(8,128)} %get-tuple-element.665), channel_id=1, source_target_pairs={{0,1},{1,2},{2,3},{3,4},{4,5},{5,6},{6,7},{7,8},{8,9},{9,10},{10,1... | collective-permute-start | bytes 196616 | tf_op jit(solution)/shard_map/while/body/eval_jaxpr/ppermute | solution.py:89
  540.8 13.1 %collective-permute-start.4 = (f32[2,32,256]{2,1,0:T(8,128)}, f32[2,32,256]{2,1,0:T(8,128)S(1)}, u32[]{:S(2)}, u32[]{:S(2)}) collective-permute-start(f32[2,32,256]{2,1,0:T(8,128)} %get-tuple-element.665), channel_id=1, source_target_pairs={{0,1},{1,2},{2,3},{3,4},{4,5},{5,6},{6,7},{7,8},{8,9},{9,10},{10,1... | collective-permute-start | bytes 196616 | tf_op jit(solution)/shard_map/while/body/eval_jaxpr/ppermute | solution.py:89
  555.2 11.9 %collective-permute-start.4 = (f32[2,32,256]{2,1,0:T(8,128)}, f32[2,32,256]{2,1,0:T(8,128)S(1)}, u32[]{:S(2)}, u32[]{:S(2)}) collective-permute-start(f32[2,32,256]{2,1,0:T(8,128)} %get-tuple-element.665), channel_id=1, source_target_pairs={{0,1},{1,2},{2,3},{3,4},{4,5},{5,6},{6,7},{7,8},{8,9},{9,10},{10,1... | collective-permute-start | bytes 196616 | tf_op jit(solution)/shard_map/while/body/eval_jaxpr/ppermute | solution.py:89
  568.4 13.1 %collective-permute-start.4 = (f32[2,32,256]{2,1,0:T(8,128)}, f32[2,32,256]{2,1,0:T(8,128)S(1)}, u32[]{:S(2)}, u32[]{:S(2)}) collective-permute-start(f32[2,32,256]{2,1,0:T(8,128)} %get-tuple-element.665), channel_id=1, source_target_pairs={{0,1},{1,2},{2,3},{3,4},{4,5},{5,6},{6,7},{7,8},{8,9},{9,10},{10,1... | collective-permute-start | bytes 196616 | tf_op jit(solution)/shard_map/while/body/eval_jaxpr/ppermute | solution.py:89
  595.0 13.1 %collective-permute-start.4 = (f32[2,32,256]{2,1,0:T(8,128)}, f32[2,32,256]{2,1,0:T(8,128)S(1)}, u32[]{:S(2)}, u32[]{:S(2)}) collective-permute-start(f32[2,32,256]{2,1,0:T(8,128)} %get-tuple-element.665), channel_id=1, source_target_pairs={{0,1},{1,2},{2,3},{3,4},{4,5},{5,6},{6,7},{7,8},{8,9},{9,10},{10,1... | collective-permute-start | bytes 196616 | tf_op jit(solution)/shard_map/while/body/eval_jaxpr/ppermute | solution.py:89
  609.4 13.1 %collective-permute-start.4 = (f32[2,32,256]{2,1,0:T(8,128)}, f32[2,32,256]{2,1,0:T(8,128)S(1)}, u32[]{:S(2)}, u32[]{:S(2)}) collective-permute-start(f32[2,32,256]{2,1,0:T(8,128)} %get-tuple-element.665), channel_id=1, source_target_pairs={{0,1},{1,2},{2,3},{3,4},{4,5},{5,6},{6,7},{7,8},{8,9},{9,10},{10,1... | collective-permute-start | bytes 196616 | tf_op jit(solution)/shard_map/while/body/eval_jaxpr/ppermute | solution.py:89
  609.4 13.1 %collective-permute-start.5 = (f32[2,32,256]{2,1,0:T(8,128)}, f32[2,32,256]{2,1,0:T(8,128)S(1)}, u32[]{:S(2)}, u32[]{:S(2)}) collective-permute-start(f32[2,32,256]{2,1,0:T(8,128)} %get-tuple-element.666), channel_id=1, source_target_pairs={{0,1},{1,2},{2,3},{3,4},{4,5},{5,6},{6,7},{7,8},{8,9},{9,10},{10,1... | collective-permute-start | bytes 196616 | tf_op jit(solution)/shard_map/while/body/eval_jaxpr/ppermute | solution.py:89
  623.8 13.1 %collective-permute-start.4 = (f32[2,32,256]{2,1,0:T(8,128)}, f32[2,32,256]{2,1,0:T(8,128)S(1)}, u32[]{:S(2)}, u32[]{:S(2)}) collective-permute-start(f32[2,32,256]{2,1,0:T(8,128)} %get-tuple-element.665), channel_id=1, source_target_pairs={{0,1},{1,2},{2,3},{3,4},{4,5},{5,6},{6,7},{7,8},{8,9},{9,10},{10,1... | collective-permute-start | bytes 196616 | tf_op jit(solution)/shard_map/while/body/eval_jaxpr/ppermute | solution.py:89
  623.8 13.1 %collective-permute-start.5 = (f32[2,32,256]{2,1,0:T(8,128)}, f32[2,32,256]{2,1,0:T(8,128)S(1)}, u32[]{:S(2)}, u32[]{:S(2)}) collective-permute-start(f32[2,32,256]{2,1,0:T(8,128)} %get-tuple-element.666), channel_id=1, source_target_pairs={{0,1},{1,2},{2,3},{3,4},{4,5},{5,6},{6,7},{7,8},{8,9},{9,10},{10,1... | collective-permute-start | bytes 196616 | tf_op jit(solution)/shard_map/while/body/eval_jaxpr/ppermute | solution.py:89
  623.8 13.1 %collective-permute-start.3 = (bf16[2,32,256]{2,1,0:T(8,128)(2,1)S(1)}, bf16[2,32,256]{2,1,0:T(8,128)(2,1)S(1)}, u32[]{:S(2)}, u32[]{:S(2)}) collective-permute-start(bf16[2,32,256]{2,1,0:T(8,128)(2,1)S(1)} %get-tuple-element.663), channel_id=1, source_target_pairs={{0,1},{1,2},{2,3},{3,4},{4,5},{5,6},{6,7},{7,8},{8,9},{9,10},{10,1... | collective-permute-start | bytes 98312 | tf_op jit(solution)/shard_map/while/body/eval_jaxpr/ppermute | solution.py:89
  638.2 13.1 %collective-permute-start.4 = (f32[2,32,256]{2,1,0:T(8,128)}, f32[2,32,256]{2,1,0:T(8,128)S(1)}, u32[]{:S(2)}, u32[]{:S(2)}) collective-permute-start(f32[2,32,256]{2,1,0:T(8,128)} %get-tuple-element.665), channel_id=1, source_target_pairs={{0,1},{1,2},{2,3},{3,4},{4,5},{5,6},{6,7},{7,8},{8,9},{9,10},{10,1... | collective-permute-start | bytes 196616 | tf_op jit(solution)/shard_map/while/body/eval_jaxpr/ppermute | solution.py:89
  638.2 13.1 %collective-permute-start.5 = (f32[2,32,256]{2,1,0:T(8,128)}, f32[2,32,256]{2,1,0:T(8,128)S(1)}, u32[]{:S(2)}, u32[]{:S(2)}) collective-permute-start(f32[2,32,256]{2,1,0:T(8,128)} %get-tuple-element.666), channel_id=1, source_target_pairs={{0,1},{1,2},{2,3},{3,4},{4,5},{5,6},{6,7},{7,8},{8,9},{9,10},{10,1... | collective-permute-start | bytes 196616 | tf_op jit(solution)/shard_map/while/body/eval_jaxpr/ppermute | solution.py:89
  638.2 13.1 %collective-permute-start.3 = (bf16[2,32,256]{2,1,0:T(8,128)(2,1)S(1)}, bf16[2,32,256]{2,1,0:T(8,128)(2,1)S(1)}, u32[]{:S(2)}, u32[]{:S(2)}) collective-permute-start(bf16[2,32,256]{2,1,0:T(8,128)(2,1)S(1)} %get-tuple-element.663), channel_id=1, source_target_pairs={{0,1},{1,2},{2,3},{3,4},{4,5},{5,6},{6,7},{7,8},{8,9},{9,10},{10,1... | collective-permute-start | bytes 98312 | tf_op jit(solution)/shard_map/while/body/eval_jaxpr/ppermute | solution.py:89
  652.6 13.7 %collective-permute-start.6 = (f32[2,32,256]{2,1,0:T(8,128)}, f32[2,32,256]{2,1,0:T(8,128)S(1)}, u32[]{:S(2)}, u32[]{:S(2)}) collective-permute-start(f32[2,32,256]{2,1,0:T(8,128)} %get-tuple-element.410), channel_id=1, source_target_pairs={{0,1},{1,2},{2,3},{3,4},{4,5},{5,6},{6,7},{7,8},{8,9},{9,10},{10,1... | collective-permute-start | bytes 196616 | tf_op jit(solution)/shard_map/ppermute | solution.py:94
  653.4 12.9 %collective-permute-start.7 = (bf16[2,32,256]{2,1,0:T(8,128)(2,1)S(1)}, bf16[2,32,256]{2,1,0:T(8,128)(2,1)S(1)}, u32[]{:S(2)}, u32[]{:S(2)}) collective-permute-start(bf16[2,32,256]{2,1,0:T(8,128)(2,1)S(1)} %convert.15), channel_id=1, source_target_pairs={{0,1},{1,2},{2,3},{3,4},{4,5},{5,6},{6,7},{7,8},{8,9},{9,10},{10,1... | collective-permute-start | bytes 98312 | tf_op jit(solution)/shard_map/ppermute | solution.py:94
  (165 other events, 1023.2 us)
where the time goes:
time: 679 us; the launch traced here: 668 us
  starting transfers between devices  330 us (49%)
  waiting for transfers between devices  269 us (40%)
  local copies, waits for them, and re-layouts  43.7 us (6%)
  matrix products  13.5 us (2%)
  other arithmetic  8.14 us (1%)
    ppermute x124, starting transfers between devices, backward_step(): lax.ppermute((key_blk, value_blk, dkey_blk, dvalue_blk), 'cp', shift_pairs)  308 us
    ppermute x62, waiting for transfers between devices, forward_step(): key_blk, value_blk = lax.ppermute((key_blk, value_blk), 'cp', shift_pairs)  195 us
    ppermute x124, waiting for transfers between devices, backward_step(): lax.ppermute((key_blk, value_blk, dkey_blk, dvalue_blk), 'cp', shift_pairs)  62.9 us
    while x186, local copies, waits for them, and re-layouts  38.7 us
    ppermute x62, starting transfers between devices, forward_step(): key_blk, value_blk = lax.ppermute((key_blk, value_blk), 'cp', shift_pairs)  21.7 us
  transfers between devices with their start and end apart: 188, of which 113 were waited for; matrix products, arithmetic and copies ran while one was open for 0% of the time, Pallas kernels for 0%

commit v1 on v0

v1 whole, which is shorter than its diff:
```python
import functools
import math

import jax
import jax.numpy as jnp
from jax import lax
from jax.experimental import pallas as pl
from jax.experimental.pallas import tpu as pltpu
from jax.sharding import PartitionSpec as P

ROPE_BASE = 10000
CORES = 2
LOG2E = math.log2(math.e)


def rope_tables(positions, head):
    half_dim = head // 2
    inv_freq = jnp.power(jnp.float32(ROPE_BASE), -2.0 * jnp.arange(half_dim, dtype=jnp.float32) / head)
    angles = positions.astype(jnp.float32)[..., None] * inv_freq
    return jnp.cos(angles), jnp.sin(angles)


def rot_halves(x1, x2, c, s):
    return x1 * c - x2 * s, x2 * c + x1 * s


def kernel(side, tokens, heads, head,
           tab_in, key_in, val_in, q_hbm, do_hbm,
           out_hbm, dq_hbm, gk_hbm, gv_hbm,
           tabs, qbuf, dobuf, kst, kbuf, vbuf, sbuf, dpbuf, dsbuf, pbf, rinv, delta, obuf, dqbuf,
           dk_part, dv_part, rk, rv, vsum, rvy, ksum, rkx, gkb, gvb,
           sem_loc, sem_px_s, sem_px_r, sem_kx, sem_ky, sem_vy, sem_vx,
           sem_dv_s, sem_dv_r, sem_dk_s, sem_dk_r, sem_dvy_s, sem_dvy_r, sem_dkx_s, sem_dkx_r,
           sem_o_s, sem_o_r):
    n = side
    half = head // 2
    blk = CORES * tokens
    tile = n * blk
    nrow = tokens * heads
    scale = head ** -0.5
    me = lax.axis_index('cp')
    k = lax.rem(me, CORES)
    chip = lax.div(me, CORES)
    x = lax.rem(chip, n)
    y = lax.div(chip, n)
    other = 1 - k

    def dev(yy, xx, kk):
        return (yy * n + xx) * CORES + kk

    partner = dev(y, x, other)

    def rcopy(src, dst, ssem, rsem, target):
        return pltpu.make_async_remote_copy(src_ref=src, dst_ref=dst, send_sem=ssem, recv_sem=rsem,
                                            device_id={'cp': target}, device_id_type=pl.DeviceIdType.MESH)

    lq = pltpu.make_async_copy(q_hbm.at[k], qbuf.at[k], sem_loc.at[0])
    ld = pltpu.make_async_copy(do_hbm.at[k], dobuf.at[k], sem_loc.at[1])
    lq.start()
    ld.start()

    bar = pltpu.get_barrier_semaphore()
    peers = [partner]
    for d in range(1, n):
        peers.append(dev(y, lax.rem(x + d, n), k))
        peers.append(dev(lax.rem(y + d, n), x, k))
    for p in peers:
        pl.semaphore_signal(bar, inc=1, device_id={'cp': p}, device_id_type=pl.DeviceIdType.MESH)

    c_own = tab_in[0]
    s_own = tab_in[1]
    for b in range(CORES):
        kf = key_in[b].astype(jnp.float32)
        r1, r2 = rot_halves(kf[:, :half], kf[:, half:], c_own, s_own)
        kst[b, :, :half] = r1.astype(jnp.bfloat16)
        kst[b, :, half:] = r2.astype(jnp.bfloat16)
    tabs[k] = tab_in[...]
    mine = pl.ds(pl.multiple_of(x * blk + k * tokens, tokens), tokens)
    kbuf[y, mine] = kst[k]
    vbuf[y, mine] = val_in[k]
    pl.semaphore_wait(bar, len(peers))

    pk = rcopy(kst.at[other], kbuf.at[y, mine], sem_px_s.at[0], sem_px_r.at[0], partner)
    pv = rcopy(val_in.at[other], vbuf.at[y, mine], sem_px_s.at[1], sem_px_r.at[1], partner)
    pt = rcopy(tab_in, tabs.at[k], sem_px_s.at[2], sem_px_r.at[2], partner)
    pq = rcopy(q_hbm.at[other], qbuf.at[k], sem_px_s.at[3], sem_px_r.at[3], partner)
    pd = rcopy(do_hbm.at[other], dobuf.at[k], sem_px_s.at[4], sem_px_r.at[4], partner)
    for cp in (pk, pv, pt, pq, pd):
        cp.start()
    pk.wait_recv()
    pv.wait_recv()

    def blk_at(i):
        return pl.ds(pl.multiple_of(i * blk, blk), blk)

    xs = blk_at(x)
    kx = []
    vx0 = []
    for d in range(1, n):
        xt = lax.rem(x + d, n)
        kx.append(rcopy(kbuf.at[y, xs], kbuf.at[y, xs], sem_kx.at[0, d - 1], sem_kx.at[1, d - 1], dev(y, xt, k)))
        vx0.append(rcopy(vbuf.at[y, xs], vbuf.at[y, xs], sem_vx.at[0, 0, d - 1], sem_vx.at[1, 0, d - 1], dev(y, xt, k)))
    for cp in kx:
        cp.start()

    def vy_copy(d):
        yt = lax.rem(y + d, n)
        return rcopy(vbuf.at[y, xs], vbuf.at[y, xs], sem_vy.at[0, d - 1], sem_vy.at[1, d - 1], dev(yt, x, k))

    def ky_copy(d):
        yt = lax.rem(y + d, n)
        return rcopy(kbuf.at[y], kbuf.at[y], sem_ky.at[0, d - 1], sem_ky.at[1, d - 1], dev(yt, x, k))

    def vx_copy(dy, d):
        ys = lax.rem(y - dy + n, n)
        xt = lax.rem(x + d, n)
        return rcopy(vbuf.at[ys, xs], vbuf.at[ys, xs], sem_vx.at[0, dy, d - 1], sem_vx.at[1, dy, d - 1], dev(y, xt, k))

    for d in range(1, n):
        @pl.when(y + d < n)
        def _(d=d):
            vy_copy(d).start()
    for cp in vx0:
        cp.start()
    for cp in kx:
        cp.wait_recv()
    for d in range(1, n):
        @pl.when(y + d < n)
        def _(d=d):
            ky_copy(d).start()
    for d in range(1, n):
        @pl.when(y - d >= 0)
        def _(d=d):
            vy_copy(d).wait_recv()
            for e in range(1, n):
                vx_copy(d, e).start()

    pt.wait_recv()
    lq.wait()
    pq.wait_recv()
    def rotate_rows(tok, carry):
        for s in range(CORES):
            rows = pl.ds(pl.multiple_of(tok * heads, heads), heads)
            c = tabs[s, 0, pl.ds(tok, 1), :]
            sn = tabs[s, 1, pl.ds(tok, 1), :]
            qf = qbuf[s, rows, :].astype(jnp.float32)
            r1, r2 = rot_halves(qf[:, :half], qf[:, half:], c, sn)
            qbuf[s, rows, :half] = r1.astype(jnp.bfloat16)
            qbuf[s, rows, half:] = r2.astype(jnp.bfloat16)
        return carry
    lax.fori_loop(0, tokens, rotate_rows, 0, unroll=4)
    ld.wait()
    pd.wait_recv()

    nt = (((1,), (1,)), ((), ()))
    tn = (((0,), (0,)), ((), ()))
    f32 = jnp.float32

    for d in range(n):
        t = lax.rem(y - d + n, n)

        @pl.when(y - d >= 0)
        def _(d=d, t=t):
            if d > 0:
                ky_copy(d).wait_recv()
            for e in range(1, n):
                vx_copy(d, e).wait_recv()
            for s in range(CORES):
                sc = lax.dot_general(qbuf[s], kbuf[t], nt, preferred_element_type=f32)
                if d == 0:
                    row_tok = (x * CORES + s) * tokens + lax.broadcasted_iota(jnp.int32, sc.shape, 0) // heads
                    sc = jnp.where(lax.broadcasted_iota(jnp.int32, sc.shape, 1) <= row_tok, sc, -jnp.inf)
                sbuf[t, s] = sc
                dpbuf[t, s] = lax.dot_general(dobuf[s], vbuf[t], nt, preferred_element_type=f32)

        if d > 0:
            @pl.when(y - d < 0)
            def _(t=t):
                sbuf[t] = jnp.full(sbuf.shape[1:], -jnp.inf, f32)
                dpbuf[t] = jnp.zeros(dpbuf.shape[1:], f32)
                kbuf[t] = jnp.zeros(kbuf.shape[1:], jnp.bfloat16)
                vbuf[t] = jnp.zeros(vbuf.shape[1:], jnp.bfloat16)

    rc = 256
    for s in range(CORES):
        def fwd_rows(i, carry, s=s):
            rows = pl.ds(pl.multiple_of(i * rc, rc), rc)
            sc = [sbuf[t, s, rows, :] for t in range(n)]
            mx = sc[0]
            for t in range(1, n):
                mx = jnp.maximum(mx, sc[t])
            mx = jnp.max(mx, axis=1, keepdims=True)
            tot = None
            acc = None
            for t in range(n):
                p = jnp.exp2((sc[t] - mx) * (scale * LOG2E))
                sbuf[t, s, rows, :] = p
                tot = p if tot is None else tot + p
                o = jnp.dot(p.astype(jnp.bfloat16), vbuf[t], preferred_element_type=f32)
                acc = o if acc is None else acc + o
            tot = jnp.sum(tot, axis=1, keepdims=True)
            inv = 1.0 / tot
            ob = (acc * inv).astype(jnp.bfloat16)
            obuf[s, rows, :] = ob
            dl = jnp.sum(ob.astype(f32) * dobuf[s, rows, :].astype(f32), axis=1, keepdims=True)
            rinv[s, rows, :] = jnp.broadcast_to(inv, (rc, 128))
            delta[s, rows, :] = jnp.broadcast_to(dl, (rc, 128))
            return carry
        lax.fori_loop(0, nrow // rc, fwd_rows, 0)

    oloc = pltpu.make_async_copy(obuf.at[k], out_hbm.at[k], sem_loc.at[2])
    orem = rcopy(obuf.at[other], out_hbm.at[k], sem_o_s.at[0], sem_o_r.at[0], partner)
    oloc.start()
    orem.start()

    def dv_copy(t, d):
        xt = lax.rem(x + d, n)
        return rcopy(dv_part.at[t, blk_at(xt)], rv.at[d - 1, t], sem_dv_s.at[t, d - 1], sem_dv_r.at[t, d - 1], dev(y, xt, k))

    def dk_copy(d):
        t = lax.rem(y - d + n, n)
        return rcopy(dk_part.at[t], rk.at[d - 1], sem_dk_s.at[d - 1], sem_dk_r.at[d - 1], dev(t, x, k))

    for t in range(n):
        for s in range(CORES):
            def bwd_rows(i, carry, s=s, t=t):
                rows = pl.ds(pl.multiple_of(i * rc, rc), rc)
                iv = rinv[s, rows, :1]
                dl = delta[s, rows, :1]
                p = sbuf[t, s, rows, :] * iv
                ds = p * (dpbuf[t, s, rows, :] - dl)
                pbf[s, rows, :] = p.astype(jnp.bfloat16)
                dsbuf[t, s, rows, :] = ds.astype(jnp.bfloat16)
                return carry
            lax.fori_loop(0, nrow // rc, bwd_rows, 0)
        dva = None
        dka = None
        for s in range(CORES):
            a = lax.dot_general(pbf[s], dobuf[s], tn, preferred_element_type=f32)
            dva = a if dva is None else dva + a
        dv_part[t] = dva

        @pl.when(y >= t)
        def _(t=t):
            for d in range(1, n):
                dv_copy(t, d).start()
        for s in range(CORES):
            a = lax.dot_general(dsbuf[t, s], qbuf[s], tn, preferred_element_type=f32)
            dka = a if dka is None else dka + a
        dk_part[t] = dka * scale

        for d in range(1, n):
            @pl.when(y == t + d)
            def _(d=d):
                dk_copy(d).start()

    for s in range(CORES):
        def dq_rows(i, carry, s=s):
            rows = pl.ds(pl.multiple_of(i * rc, rc), rc)
            acc = None
            for t in range(n):
                a = jnp.dot(dsbuf[t, s, rows, :], kbuf[t], preferred_element_type=f32)
                acc = a if acc is None else acc + a
            acc = acc * scale
            for j in range(rc // heads):
                tok = i * (rc // heads) + j
                c = tabs[s, 0, pl.ds(tok, 1), :]
                sn = tabs[s, 1, pl.ds(tok, 1), :]
                g = acc[j * heads:(j + 1) * heads]
                r1, r2 = rot_halves(g[:, :half], g[:, half:], c, -sn)
                orow = pl.ds(pl.multiple_of(tok * heads, heads), heads)
                dqbuf[s, orow, :half] = r1.astype(jnp.bfloat16)
                dqbuf[s, orow, half:] = r2.astype(jnp.bfloat16)
            return carry
        lax.fori_loop(0, nrow // rc, dq_rows, 0)
    qloc = pltpu.make_async_copy(dqbuf.at[k], dq_hbm.at[k], sem_loc.at[3])
    qrem = rcopy(dqbuf.at[other], dq_hbm.at[k], sem_o_s.at[1], sem_o_r.at[1], partner)
    qloc.start()
    qrem.start()

    def dvy_copy(d):
        t = lax.rem(y - d + n, n)
        return rcopy(vsum.at[t], rvy.at[d - 1], sem_dvy_s.at[d - 1], sem_dvy_r.at[d - 1], dev(t, x, k))

    def dkx_copy(d):
        xt = lax.rem(x + d, n)
        return rcopy(ksum.at[blk_at(xt)], rkx.at[d - 1], sem_dkx_s.at[d - 1], sem_dkx_r.at[d - 1], dev(y, xt, k))

    for t in range(n):
        @pl.when(y >= t)
        def _(t=t):
            acc = dv_part[t, xs, :]
            for d in range(1, n):
                dv_copy(t, d).wait_recv()
                acc = acc + rv[d - 1, t]
            vsum[t] = acc
        for d in range(1, n):
            @pl.when(y == t + d)
            def _(d=d):
                dvy_copy(d).start()

    ksum[...] = dk_part[y]
    for d in range(1, n):
        @pl.when(y + d < n)
        def _(d=d):
            dk_copy(d).wait_recv()
            ksum[...] += rk[d - 1]
    for d in range(1, n):
        dkx_copy(d).start()

    rvsum = vsum.at[y]
    for d in range(1, n):
        @pl.when(y + d < n)
        def _(d=d):
            dvy_copy(d).wait_recv()
            vsum[y] += rvy[d - 1]
    gv = vsum[y]
    gk = ksum[xs, :]
    for d in range(1, n):
        dkx_copy(d).wait_recv()
        gk = gk + rkx[d - 1]
    for s in range(CORES):
        gvb[s] = gv[s * tokens:(s + 1) * tokens].astype(jnp.bfloat16)
        g = gk[s * tokens:(s + 1) * tokens]
        r1, r2 = rot_halves(g[:, :half], g[:, half:], tabs[s, 0], -tabs[s, 1])
        gkb[s, :, :half] = r1.astype(jnp.bfloat16)
        gkb[s, :, half:] = r2.astype(jnp.bfloat16)
    gkl = pltpu.make_async_copy(gkb.at[k], gk_hbm.at[k], sem_loc.at[4])
    gvl = pltpu.make_async_copy(gvb.at[k], gv_hbm.at[k], sem_loc.at[5])
    gkr = rcopy(gkb.at[other], gk_hbm.at[k], sem_o_s.at[2], sem_o_r.at[2], partner)
    gvr = rcopy(gvb.at[other], gv_hbm.at[k], sem_o_s.at[3], sem_o_r.at[3], partner)
    for cp in (gkl, gvl, gkr, gvr):
        cp.start()

    for cp in (pk, pv, pt, pq, pd):
        cp.wait_send()
    for cp in kx + vx0:
        cp.wait_send()
    for d in range(1, n):
        @pl.when(y + d < n)
        def _(d=d):
            vy_copy(d).wait_send()
            ky_copy(d).wait_send()

        @pl.when(y - d >= 0)
        def _(d=d):
            for e in range(1, n):
                vx_copy(d, e).wait_send()
            dk_copy(d).wait_send()
            dvy_copy(d).wait_send()
        dkx_copy(d).wait_send()
    for t in range(n):
        @pl.when(y >= t)
        def _(t=t):
            for d in range(1, n):
                dv_copy(t, d).wait_send()
    for cp in (oloc, qloc, gkl, gvl):
        cp.wait()
    for cp in (orem, qrem, gkr, gvr):
        cp.wait()


def solution(mesh):
    cp_size = mesh.shape['cp']
    side = math.isqrt(cp_size // CORES)
    query_spec = P('dp', 'cp', None, None)
    kv_spec = P('dp', 'cp', None)
    pos_spec = P(('dp', 'cp'))

    def per_device(query, key, value, positions, grad_out):
        batch, tokens, heads, head = query.shape
        nrow = tokens * heads
        tab = jnp.stack(rope_tables(positions, head))
        q2 = query.reshape(batch, nrow, head)
        d2 = grad_out.reshape(batch, nrow, head)
        n = side
        blk = CORES * tokens
        tile = n * blk
        bf16, f32 = jnp.bfloat16, jnp.float32
        V = pltpu.VMEM
        D = pltpu.SemaphoreType.DMA
        scratch = [
            V((CORES, 2, tokens, head // 2), f32),
            V((CORES, nrow, head), bf16),
            V((CORES, nrow, head), bf16),
            V((CORES, tokens, head), bf16),
            V((n, tile, head), bf16),
            V((n, tile, head), bf16),
            V((n, CORES, nrow, tile), f32),
            V((n, CORES, nrow, tile), f32),
            V((n, CORES, nrow, tile), bf16),
            V((CORES, nrow, tile), bf16),
            V((CORES, nrow, 128), f32),
            V((CORES, nrow, 128), f32),
            V((CORES, nrow, head), bf16),
            V((CORES, nrow, head), bf16),
            V((n, tile, head), f32),
            V((n, tile, head), f32),
            V((n - 1, tile, head), f32),
            V((n - 1, n, blk, head), f32),
            V((n, blk, head), f32),
            V((n - 1, blk, head), f32),
            V((tile, head), f32),
            V((n - 1, blk, head), f32),
            V((CORES, tokens, head), bf16),
            V((CORES, tokens, head), bf16),
            D((6,)), D((5,)), D((5,)),
            D((2, n - 1)), D((2, n - 1)), D((2, n - 1)), D((2, n, n - 1)),
            D((n, n - 1)), D((n, n - 1)), D((n - 1,)), D((n - 1,)),
            D((n - 1,)), D((n - 1,)), D((n - 1,)), D((n - 1,)),
            D((4,)), D((4,)),
        ]
        vmem = pl.BlockSpec(memory_space=pltpu.VMEM)
        hbm = pl.BlockSpec(memory_space=pl.ANY)
        out, dq, gk, gv = pl.pallas_call(
            functools.partial(kernel, side, tokens, heads, head),
            out_shape=[jax.ShapeDtypeStruct(q2.shape, bf16), jax.ShapeDtypeStruct(q2.shape, bf16),
                       jax.ShapeDtypeStruct(key.shape, bf16), jax.ShapeDtypeStruct(key.shape, bf16)],
            in_specs=[vmem, vmem, vmem, hbm, hbm],
            out_specs=[hbm, hbm, hbm, hbm],
            scratch_shapes=scratch,
            compiler_params=pltpu.CompilerParams(collective_id=0, has_side_effects=True,
                                                 vmem_limit_bytes=60 * 1024 * 1024),
        )(tab, key, value, q2, d2)
        return out.reshape(query.shape), dq.reshape(query.shape), gk, gv

    return jax.shard_map(per_device, mesh=mesh, in_specs=(query_spec, kv_spec, kv_spec, pos_spec, query_spec),
                         out_specs=(query_spec, query_spec, kv_spec, kv_spec), check_vma=False)
```

time: 679 us -> 57.7 us (0.08); the launches traced: 668 us -> 57.4 us
  starting transfers between devices: 330 us -> 0 us
  waiting for transfers between devices: 269 us -> 0 us
  Pallas kernels: 0 us -> 50.6 us
  local copies, waits for them, and re-layouts: 43.7 us -> 5.36 us
  matrix products: 13.5 us -> 0 us
  other arithmetic: 8.14 us -> 0.78 us
    ppermute x188 -> x0, starting transfers between devices: 330 us -> none  [the longest x124 308 us: backward_step(): lax.ppermute((key_blk, value_blk, dkey_blk, dvalue_blk), 'cp', shift_pairs)]
    ppermute x188 -> x0, waiting for transfers between devices: 269 us -> none  [the longest x62 195 us: forward_step(): key_blk, value_blk = lax.ppermute((key_blk, value_blk), 'cp', shift_pairs)]
    pallas_call x0 -> x1, Pallas kernels: none -> 50.6 us  [per_device(): pl.pallas_call(functools.partial(kernel, side, tokens, heads, head), out_...]
    while x188 -> x0, local copies, waits for them, and re-layouts: 40.8 us -> none
    dot_general x13 -> x0, matrix products: 13.5 us -> none  [the longest x3 4.05 us: block_scores(): jnp.einsum('crie,cle->cril', query_rot, key_blk, preferred_element_type=j...]
  transfers between devices with their start and end apart: 188 -> 0, of which waited for: 113 -> 0; matrix products, arithmetic and copies ran while one was open for 0% -> 0% of each run, Pallas kernels for 0% -> 0%
where the time goes in v1:
time: 57.7 us; the launch traced here: 57.4 us
  Pallas kernels  50.6 us (88%)
  local copies, waits for them, and re-layouts  5.36 us (9%)
  other arithmetic  0.78 us (1%)
  between operations  0.67 us (1%)
    pallas_call x1, Pallas kernels, per_device(): pl.pallas_call(functools.partial(kernel, side, tokens, heads, head), out_...  50.6 us
    unnamed x12, local copies, waits for them, and re-layouts  5.36 us

profile of v1, /device:TPU:97, one launch (start us, length us, event | category | flops | bytes accessed | tf_op | source)
XLA Modules:
  0.0 57.4 jit_solution(9565517068827999122)
XLA Ops:
  0.6 0.0 copy-start.3
  0.6 0.6 %copy-done.3 = s32[32]{0:T(128)S(1)} copy-done((s32[32]{0:T(128)S(1)}, s32[32]{0:T(128)}, u32[]{:S(2)}) %copy-start.3) | copy-done | bytes 152
  1.3 0.1 multiply_cosine_fusion
  1.4 0.6 %pad_maximum_fusion.tab_in = f32[2,32,128]{2,1,0:T(8,128)} fusion(f32[1,32,128]{2,1,0:T(8,128)S(1)} %get-tuple-element.13, f32[1,32,128]{2,1,0:T(8,128)S(1)} %get-tuple-element.12), kind=kLoop, calls=%fused_computation | loop fusion | flops 8192 | bytes 65536 | tf_op jit(solution)/shard_map/stack | solution.py:373
  2.1 50.6 %shard_map.84 = (bf16[2,1024,256]{2,1,0:T(8,128)(2,1)}, bf16[2,1024,256]{2,1,0:T(8,128)(2,1)}, bf16[2,32,256]{2,1,0:T(8,128)(2,1)}, bf16[2,32,256]{2,1,0:T(8,128)(2,1)}) custom-call(f32[2,32,128]{2,1,0:T(8,128)} %pad_maximum_fusion.tab_in, bf16[2,32,256]{2,1,0:T(8,128)(2,1)} %key_in.1, bf16[2,32,256]{2,1,0:T(8,128)(2,1)} %val_in.1, ...), custom_call_target="tpu_custom_call" | custom-call | tf_op jit(solution)/shard_map/pallas_call | solution.py:415
  52.7 0.0 copy-start
  52.7 2.4 %copy.13 = bf16[2,32,32,256]{3,2,1,0:T(8,128)(2,1)} copy(bf16[2,32,32,256]{3,2,1,0:T(8,128)(2,1)} %bitcast.7) | data formatting | bytes 2097152
  55.0 0.0 copy-done
  55.1 0.0 copy-start.2
  55.1 1.0 %copy.14 = bf16[2,32,32,256]{3,2,1,0:T(8,128)(2,1)} copy(bf16[2,32,32,256]{3,2,1,0:T(8,128)(2,1)S(1)} %bitcast.6) | data formatting | bytes 2097152
  56.0 0.0 copy-done.2
  56.0 0.0 copy-start.1
  56.0 0.6 %copy.15 = bf16[2,32,256]{2,1,0:T(8,128)(2,1)} copy(bf16[2,32,256]{2,1,0:T(8,128)(2,1)S(1)} %copy-done.2) | data formatting | bytes 65536
  56.6 0.2 copy-done.1
  56.8 0.6 %copy.16 = bf16[2,32,256]{2,1,0:T(8,128)(2,1)} copy(bf16[2,32,256]{2,1,0:T(8,128)(2,1)S(1)} %copy-done.1) | data formatting | bytes 65536
  (2 shorter events, 0.0 us)
Async XLA Ops:
  0.6 0.7 %copy-start.3 = (s32[32]{0:T(128)S(1)}, s32[32]{0:T(128)}, u32[]{:S(2)}) copy-start(s32[32]{0:T(128)} %param.8) | copy-start | bytes 388
  52.7 2.4 %copy-start = (bf16[2,1024,256]{2,1,0:T(8,128)(2,1)S(1)}, bf16[2,1024,256]{2,1,0:T(8,128)(2,1)}, u32[]{:S(2)}) copy-start(bf16[2,1024,256]{2,1,0:T(8,128)(2,1)} %get-tuple-element.9) | copy-start | bytes 3145732
  55.1 1.0 %copy-start.2 = (bf16[2,32,256]{2,1,0:T(8,128)(2,1)S(1)}, bf16[2,32,256]{2,1,0:T(8,128)(2,1)}, u32[]{:S(2)}) copy-start(bf16[2,32,256]{2,1,0:T(8,128)(2,1)} %get-tuple-element.20) | copy-start | bytes 98308
  56.0 0.8 %copy-start.1 = (bf16[2,32,256]{2,1,0:T(8,128)(2,1)S(1)}, bf16[2,32,256]{2,1,0:T(8,128)(2,1)}, u32[]{:S(2)}) copy-start(bf16[2,32,256]{2,1,0:T(8,128)(2,1)} %get-tuple-element.21) | copy-start | bytes 98308

commit v2 on v0

v2 whole, which is shorter than its diff:
```python
import functools
import math

import jax
import jax.numpy as jnp
from jax import lax
from jax.experimental import pallas as pl
from jax.experimental.pallas import tpu as pltpu
from jax.sharding import PartitionSpec as P

ROPE_BASE = 10000
CORES = 2
SIDE = 4
LOG2E = math.log2(math.e)
TILE_ORDER = (1, 0, 2, 3)

KEY_MSGS = (
    (0, 0, 0, 1, 0, None), (0, 0, None, 3, 2, None), (0, 0, 1, 1, 1, None),
    (1, 1, 1, 0, 0, None), (1, 1, 0, 2, 0, None), (1, 1, 1, 2, 3, None),
    (2, 2, None, 3, 0, None),
    (0, 1, 1, 3, 3, 0), (1, 0, 0, 2, 1, 0), (1, 0, 1, 2, 2, 1), (2, 1, 0, 3, 1, 0),
)
KEY_SLOTS = {(1, 0): (0, 1), (2, 1): (0, 3), (2, 0): (1, 2), (3, 2): (0,), (3, 1): (1, 3), (3, 0): (2,)}

DK_MSGS = (
    (3, 1, 0, 2, 0, None), (3, 1, 1, 0, 0, None), (2, 1, 1, 1, 2, None),
    (3, 0, 1, 0, 2, None), (2, 0, 0, 3, 0, None), (2, 0, 1, 1, 0, None), (1, 0, 0, 0, 3, None),
    (3, 2, 0, 2, 1, None), (3, 2, 1, 2, 2, None),
    (3, 0, 0, 0, 1, 0), (2, 1, 0, 1, 1, 0), (1, 0, 1, 0, 4, 0),
)
DK_FINAL = ((2, 0, (1,)), (2, 1, (2,)), (1, 0, (1,)), (1, 1, (2, 3)), (0, 0, (1, 3)), (0, 1, (2, 4)))


def rope_tables(positions, head):
    half_dim = head // 2
    inv_freq = jnp.power(jnp.float32(ROPE_BASE), -2.0 * jnp.arange(half_dim, dtype=jnp.float32) / head)
    angles = positions.astype(jnp.float32)[..., None] * inv_freq
    return jnp.cos(angles), jnp.sin(angles)


def rot_halves(x1, x2, c, s):
    return x1 * c - x2 * s, x2 * c + x1 * s


def kernel(tokens, heads, head,
           tab_in, key_in, val_in, q_hbm, do_hbm,
           out_ref, dq_ref, gk_ref, gv_ref,
           tabs, qbuf, dobuf, kst, kbuf, vbuf, krel, sbuf, dpbuf, dsbuf, mbuf, lbuf, lse, delta, oacc, obuf, dqbuf,
           dk_part, dv_part, rk, rv, vsum, rvy, rkx,
           sem_loc, sem_px, sem_kx, sem_vy, sem_vx, sem_ky_s, sem_ky_r,
           sem_dv_s, sem_dv_r, sem_dk_s, sem_dk_r, sem_fv_s, sem_fv_r, sem_fk_s, sem_fk_r, sem_o):
    n = SIDE
    half = head // 2
    blk = CORES * tokens
    tile = n * blk
    ht = tile // 2
    nrow = tokens * heads
    scale = head ** -0.5
    c2 = scale * LOG2E
    f32, bf16 = jnp.float32, jnp.bfloat16
    me = lax.axis_index('cp')
    k = lax.rem(me, CORES)
    chip = lax.div(me, CORES)
    x = lax.rem(chip, n)
    y = lax.div(chip, n)
    other = 1 - k
    xr = lax.rem(x + 1, n)
    xo = lax.rem(x + 2, n)
    xl = lax.rem(x + 3, n)

    def dev(yy, xx, kk):
        return (yy * n + xx) * CORES + kk

    partner = dev(y, x, other)
    right, left = dev(y, xr, k), dev(y, xl, k)

    def rcopy(src, dst, ssem, rsem, target):
        return pltpu.make_async_remote_copy(src_ref=src, dst_ref=dst, send_sem=ssem, recv_sem=rsem,
                                            device_id={'cp': target}, device_id_type=pl.DeviceIdType.MESH)

    def at(i, size):
        return pl.ds(pl.multiple_of(i * size, size), size)

    lq = pltpu.make_async_copy(q_hbm.at[k], qbuf.at[k], sem_loc.at[0])
    ld = pltpu.make_async_copy(do_hbm.at[k], dobuf.at[k], sem_loc.at[1])
    lq.start()
    ld.start()
    bar = pltpu.get_barrier_semaphore()
    peers = [partner]
    for d in range(1, n):
        for b in range(CORES):
            peers.append(dev(y, lax.rem(x + d, n), b))
            peers.append(dev(lax.rem(y + d, n), x, b))
    for p in peers:
        pl.semaphore_signal(bar, inc=1, device_id={'cp': p}, device_id_type=pl.DeviceIdType.MESH)

    for b in range(CORES):
        kf = key_in[b].astype(f32)
        r1, r2 = rot_halves(kf[:, :half], kf[:, half:], tab_in[0], tab_in[1])
        kst[b, :, :half] = r1.astype(bf16)
        kst[b, :, half:] = r2.astype(bf16)
    tabs[k] = tab_in[...]
    mine = at(x * CORES + k, tokens)
    kbuf[y, mine] = kst[k]
    vbuf[y, mine] = val_in[k]
    pl.semaphore_wait(bar, len(peers))
    pk = rcopy(kst.at[other], kbuf.at[y, mine], sem_px.at[0, 0], sem_px.at[1, 0], partner)
    pv = rcopy(val_in.at[other], vbuf.at[y, mine], sem_px.at[0, 1], sem_px.at[1, 1], partner)
    pt = rcopy(tab_in, tabs.at[k], sem_px.at[0, 2], sem_px.at[1, 2], partner)
    pq = rcopy(q_hbm.at[other], qbuf.at[k], sem_px.at[0, 3], sem_px.at[1, 3], partner)
    pd = rcopy(do_hbm.at[other], dobuf.at[k], sem_px.at[0, 4], sem_px.at[1, 4], partner)

    def kx_copy(d, b, src_core=None):
        return rcopy(kst.at[b], kbuf.at[y, mine], sem_kx.at[0, d - 1, b],
                     sem_kx.at[1, d - 1, k if src_core is None else src_core], dev(y, lax.rem(x + d, n), b))

    def vy_copy(d, b, src_core=None):
        return rcopy(val_in.at[b], vbuf.at[y, mine], sem_vy.at[0, d - 1, b],
                     sem_vy.at[1, d - 1, k if src_core is None else src_core], dev(lax.rem(y + d, n), x, b))

    pv.start()
    pk.start()
    for d in (2, 1, 3):
        for b in range(CORES):
            kx_copy(d, b).start()
    for d in (2, 1, 3):
        @pl.when(y + d < n)
        def _(d=d):
            for b in range(CORES):
                vy_copy(d, b).start()
    pt.start()
    pq.start()
    pd.start()

    def vx_copy(dy, i):
        t = lax.rem(y - dy + n, n)
        if i == 0:
            ref, target = vbuf.at[t, at(x, blk)], right
        elif i == 1:
            ref, target = vbuf.at[t, at(x, blk)], left
        elif i == 2:
            ref, target = vbuf.at[t, at(xl * CORES, tokens)], right
        else:
            ref, target = vbuf.at[t, at(xr * CORES + 1, tokens)], left
        return rcopy(ref, ref, sem_vx.at[0, dy, i], sem_vx.at[1, dy, i], target)

    def vx_relay(dy):
        vx_copy(dy, 0).wait_recv()
        vx_copy(dy, 2).start()
        vx_copy(dy, 1).wait_recv()
        vx_copy(dy, 3).start()

    def key_copy(i):
        src, t, hf, dst, slot, after = KEY_MSGS[i]
        ref = kbuf.at[t] if hf is None else kbuf.at[t, pl.ds(hf * ht, ht)]
        s_ref = krel if (src == 0 and after is not None) else ref
        d_ref = krel if dst == 0 else ref
        return rcopy(s_ref, d_ref, sem_ky_s.at[i], sem_ky_r.at[slot], dev(dst, x, k))

    def key_wait(row, slot):
        for i, m in enumerate(KEY_MSGS):
            if m[3] == row and m[4] == slot:
                key_copy(i).wait_recv()
    pv.wait_recv()
    vx_copy(0, 0).start()
    vx_copy(0, 1).start()
    pk.wait_recv()
    for d in range(1, n):
        for b in range(CORES):
            kx_copy(d, b, b).wait_recv()
    for r in range(n):
        @pl.when(y == r)
        def _(r=r):
            for i, m in enumerate(KEY_MSGS):
                if m[0] == r and m[5] is None:
                    key_copy(i).start()
    for d in range(1, n):
        @pl.when(y - d >= 0)
        def _(d=d):
            for b in range(CORES):
                vy_copy(d, b, b).wait_recv()
            vx_copy(d, 0).start()
            vx_copy(d, 1).start()
    pt.wait_recv()
    lq.wait()
    pq.wait_recv()
    def rotate_rows(tok, carry):
        for s in range(CORES):
            rows = at(tok, heads)
            c = tabs[s, 0, pl.ds(tok, 1), :]
            sn = tabs[s, 1, pl.ds(tok, 1), :]
            qf = qbuf[s, rows, :].astype(f32)
            r1, r2 = rot_halves(qf[:, :half], qf[:, half:], c, sn)
            qbuf[s, rows, :half] = r1.astype(bf16)
            qbuf[s, rows, half:] = r2.astype(bf16)
        return carry
    lax.fori_loop(0, tokens, rotate_rows, 0, unroll=4)
    ld.wait()
    pd.wait_recv()
    vx_relay(0)
    vx_copy(0, 2).wait_recv()
    vx_copy(0, 3).wait_recv()

    nt = (((1,), (1,)), ((), ()))
    tn = (((0,), (0,)), ((), ()))

    rf = 1024

    def forward_tile(t, first):
        kt = kbuf.at[t]
        vt = vbuf.at[t]

        def rows_body(i, carry):
            for s in range(CORES):
                rows = at(i, rf)
                sc = lax.dot_general(qbuf[s, rows, :], kt[...], nt, preferred_element_type=f32)
                if first:
                    row_tok = (x * CORES + s) * tokens + (i * rf + lax.broadcasted_iota(jnp.int32, sc.shape, 0)) // heads
                    sc = jnp.where(lax.broadcasted_iota(jnp.int32, sc.shape, 1) <= row_tok, sc, -jnp.inf)
                sbuf[t, s, rows, :] = sc
                mx = jnp.max(sc, axis=1, keepdims=True)
                if not first:
                    old = mbuf[s, rows, :]
                    mx = jnp.maximum(old, mx)
                    fac = jnp.exp2((old - mx) * c2)
                else:
                    mx = jnp.broadcast_to(mx, (rf, 128))
                mbuf[s, rows, :] = mx
                mxw = jnp.concatenate([mx] * (tile // 128), axis=1)
                p = jnp.exp2((sc - mxw) * c2)
                tot = p[:, :128] + p[:, 128:]
                o = jnp.dot(p.astype(bf16), vt[...], preferred_element_type=f32)
                if not first:
                    tot = tot + lbuf[s, rows, :] * fac
                    o = o + oacc[s, rows, :] * jnp.concatenate([fac] * (head // 128), axis=1)
                lbuf[s, rows, :] = tot
                oacc[s, rows, :] = o
                dpbuf[t, s, rows, :] = lax.dot_general(dobuf[s, rows, :], vt[...], nt, preferred_element_type=f32)
            return carry
        if nrow == rf:
            rows_body(0, 0)
        else:
            lax.fori_loop(0, nrow // rf, rows_body, 0)
    forward_tile(y, True)
    for d in range(1, n):
        @pl.when(y - d >= 0)
        def _(d=d):
            vx_relay(d)
    for r in range(n - 1):
        @pl.when(y == r)
        def _(r=r):
            for i, m in enumerate(KEY_MSGS):
                if m[0] == r and m[5] is not None:
                    key_wait(r, m[5])
                    key_copy(i).start()
    for j, d in enumerate((1, n - 1, 2)):
        dd = jnp.where(y == n - 1, d, j + 1)

        @pl.when(y - (j + 1) >= 0)
        def _(j=j, d=d, dd=dd):
            t = y - dd
            for r in range(n):
                tr = r - (d if r == n - 1 else j + 1)
                if tr < 0:
                    continue

                @pl.when(y == r)
                def _(r=r, tr=tr):
                    for slot in KEY_SLOTS[(r, tr)]:
                        if not any(m[0] == r and m[5] == slot for m in KEY_MSGS):
                            key_wait(r, slot)
                    vx_copy(r - tr, 2).wait_recv()
                    vx_copy(r - tr, 3).wait_recv()
            forward_tile(t, False)
    rc = 256
    for s in range(CORES):
        def out_rows(i, carry, s=s):
            rows = at(i, rc)
            tot = jnp.sum(lbuf[s, rows, :], axis=1, keepdims=True)
            inv = 1.0 / tot
            ob = (oacc[s, rows, :] * inv).astype(bf16)
            obuf[s, rows, :] = ob
            dl = jnp.sum(ob.astype(f32) * dobuf[s, rows, :].astype(f32), axis=1, keepdims=True)
            lse[s, rows, :] = mbuf[s, rows, :] * c2 + jnp.broadcast_to(jnp.log2(tot), (rc, 128))
            delta[s, rows, :] = jnp.broadcast_to(dl, (rc, 128))
            return carry
        lax.fori_loop(0, nrow // rc, out_rows, 0, unroll=2)
    oloc = pltpu.make_async_copy(obuf.at[k], out_ref.at[k], sem_loc.at[2])
    orem = rcopy(obuf.at[other], out_ref.at[k], sem_o.at[0, 0], sem_o.at[1, 0], partner)
    oloc.start()
    orem.start()

    def dv_copy(t, i):
        xt = (xo, xr, xr, xo, xl, xl)[i]
        hf = (0, 1, 0, 1, 0, 1)[i]
        return rcopy(dv_part.at[t, at(xt * CORES + hf, tokens)], rv.at[t, i], sem_dv_s.at[t, i], sem_dv_r.at[t, i],
                     right if i < 3 else left)

    def dv_combine(t):
        for i in (0, 3):
            dv_copy(t, i).wait_recv()
            rows = at(xr * CORES, tokens) if i == 0 else at(xl * CORES + 1, tokens)
            dv_part[t, rows] = dv_part[t, rows] + rv[t, i]
            dv_copy(t, i + 2).start()

    def dk_copy(i):
        src, t, hf, dst, slot, after = DK_MSGS[i]
        return rcopy(dk_part.at[t, pl.ds(hf * ht, ht)], rk.at[slot], sem_dk_s.at[i], sem_dk_r.at[slot], dev(dst, x, k))

    dk_relay = rcopy(rk.at[0], rk.at[3], sem_dk_s.at[len(DK_MSGS)], sem_dk_r.at[3], dev(1, x, k))

    def dk_wait(slot):
        rcopy(rk.at[slot], rk.at[slot], sem_dk_s.at[0], sem_dk_r.at[slot], partner).wait_recv()

    def fv_copy(t, c):
        dst = dev(t, x, c)
        return rcopy(vsum.at[t, c], rvy.at[y - t, k], sem_fv_s.at[t, c], sem_fv_r.at[y - t, k], dst)

    def fv_own():
        return rcopy(vsum.at[y, other], rvy.at[0, k], sem_fv_s.at[y, other], sem_fv_r.at[0, k], partner)

    def fk_copy(d, c, src_core=None):
        xt = lax.rem(x + d, n)
        return rcopy(dk_part.at[y, at(xt * CORES + c, tokens)], rkx.at[d, k], sem_fk_s.at[d, c],
                     sem_fk_r.at[d, k if src_core is None else src_core], dev(y, xt, c))

    def fk_own(src_core=None):
        return rcopy(dk_part.at[y, at(x * CORES + other, tokens)], rkx.at[0, k], sem_fk_s.at[0, 0],
                     sem_fk_r.at[0, k if src_core is None else src_core], partner)

    def fk_start():
        for d in (2, 1, 3):
            for c in range(CORES):
                fk_copy(d, c).start()
        fk_own().start()

    rb = 512

    for idx, t in enumerate(TILE_ORDER):
        @pl.when(y >= t)
        def _(t=t):
            dva = None
            dka = None
            for s in range(CORES):
                for i in range(nrow // rb):
                    rows = pl.ds(i * rb, rb)
                    ls = lse[s, rows, :]
                    dl = delta[s, rows, :]
                    p = jnp.exp2(sbuf[t, s, rows, :] * c2 - jnp.concatenate([ls] * (tile // 128), axis=1))
                    ds = (p * (dpbuf[t, s, rows, :] - jnp.concatenate([dl] * (tile // 128), axis=1))).astype(bf16)
                    dsbuf[t, s, rows, :] = ds
                    a = lax.dot_general(p.astype(bf16), dobuf[s, rows, :], tn, preferred_element_type=f32)
                    dva = a if dva is None else dva + a
                    a = lax.dot_general(ds, qbuf[s, rows, :], tn, preferred_element_type=f32)
                    dka = a if dka is None else dka + a
            dv_part[t] = dva
            dk_part[t] = dka * scale
            for i in (0, 3, 1, 4):
                dv_copy(t, i).start()

        @pl.when(y < t)
        def _(t=t):
            dsbuf[t] = jnp.zeros(dsbuf.shape[1:], bf16)
            kbuf[t] = jnp.zeros(kbuf.shape[1:], bf16)

        for r in range(n):
            @pl.when(y == r)
            def _(r=r, t=t):
                for i, m in enumerate(DK_MSGS):
                    if m[0] == r and m[1] == t and m[5] is None:
                        dk_copy(i).start()
        if idx > 0:
            tp = TILE_ORDER[idx - 1]

            @pl.when(y >= tp)
            def _(tp=tp):
                dv_combine(tp)
        if t == 2:
            @pl.when(y == 0)
            def _():
                dk_wait(0)
                dk_relay.start()
            for r in range(1, n):
                @pl.when(y == r)
                def _(r=r):
                    for i, m in enumerate(DK_MSGS):
                        if m[0] == r and m[5] is not None:
                            dk_wait(m[5])
                            dk_part[m[1], pl.ds(m[2] * ht, ht)] = dk_part[m[1], pl.ds(m[2] * ht, ht)] + rk[m[5]]
                            dk_copy(i).start()
    @pl.when(y == n - 1)
    def _():
        fk_start()
        dv_combine(TILE_ORDER[n - 1])
    for s in range(CORES):
        def dq_rows(i, carry, s=s):
            rows = at(i, rc)
            acc = None
            for t in range(n):
                a = jnp.dot(dsbuf[t, s, rows, :], kbuf[t], preferred_element_type=f32)
                acc = a if acc is None else acc + a
            acc = acc * scale
            for j in range(rc // heads):
                tok = i * (rc // heads) + j
                c = tabs[s, 0, pl.ds(tok, 1), :]
                sn = tabs[s, 1, pl.ds(tok, 1), :]
                g = acc[j * heads:(j + 1) * heads]
                r1, r2 = rot_halves(g[:, :half], g[:, half:], c, -sn)
                orow = at(tok, heads)
                dqbuf[s, orow, :half] = r1.astype(bf16)
                dqbuf[s, orow, half:] = r2.astype(bf16)
            return carry
        lax.fori_loop(0, nrow // rc, dq_rows, 0, unroll=2)
    qloc = pltpu.make_async_copy(dqbuf.at[k], dq_ref.at[k], sem_loc.at[3])
    qrem = rcopy(dqbuf.at[other], dq_ref.at[k], sem_o.at[0, 1], sem_o.at[1, 1], partner)
    qloc.start()
    qrem.start()
    for t in TILE_ORDER:
        @pl.when(y >= t)
        def _(t=t):
            for i in (1, 2, 4, 5):
                dv_copy(t, i).wait_recv()
            own = at(x * CORES, tokens)
            own2 = at(x * CORES + 1, tokens)
            vsum[t, 0] = dv_part[t, own] + rv[t, 2] + rv[t, 4]
            vsum[t, 1] = dv_part[t, own2] + rv[t, 1] + rv[t, 5]

        @pl.when(y > t)
        def _(t=t):
            for c in range(CORES):
                fv_copy(t, c).start()
    fv_own().start()
    for r in range(n - 1):
        @pl.when(y == r)
        def _(r=r):
            for row, hf, slots in DK_FINAL:
                if row == r:
                    acc = dk_part[r, pl.ds(hf * ht, ht)]
                    for slot in slots:
                        dk_wait(slot)
                        acc = acc + rk[slot]
                    dk_part[r, pl.ds(hf * ht, ht)] = acc
            fk_start()
    def fv_wait(d, b):
        rcopy(rvy.at[d, b], rvy.at[d, b], sem_fv_s.at[0, 0], sem_fv_r.at[d, b], partner).wait_recv()

    fv_wait(0, other)
    rvy[0, k] = vsum[y, k]
    for d in range(1, n):
        @pl.when(y + d < n)
        def _(d=d):
            for b in range(CORES):
                fv_wait(d, b)
                rvy[0, b] = rvy[0, b] + rvy[d, b]
    for b in range(CORES):
        gv_ref[b] = rvy[0, b].astype(bf16)
    fk_own(other).wait_recv()
    rkx[0, k] = dk_part[y, at(x * CORES + k, tokens)]
    for d in range(1, n):
        for b in range(CORES):
            fk_copy(d, 0, b).wait_recv()
    ct, st = tab_in[0], tab_in[1]
    for b in range(CORES):
        g = rkx[0, b] + rkx[1, b] + rkx[2, b] + rkx[3, b]
        r1, r2 = rot_halves(g[:, :half], g[:, half:], ct, -st)
        gk_ref[b, :, :half] = r1.astype(bf16)
        gk_ref[b, :, half:] = r2.astype(bf16)
    for cp in (pk, pv, pt, pq, pd):
        cp.wait_send()
    for d in range(1, n):
        for b in range(CORES):
            kx_copy(d, b).wait_send()
            fk_copy(d, b).wait_send()

        @pl.when(y + d < n)
        def _(d=d):
            for b in range(CORES):
                vy_copy(d, b).wait_send()
    fk_own().wait_send()
    fv_own().wait_send()
    for d in range(n):
        @pl.when(y - d >= 0)
        def _(d=d):
            for i in range(4):
                vx_copy(d, i).wait_send()
    for r in range(n):
        @pl.when(y == r)
        def _(r=r):
            for i, m in enumerate(KEY_MSGS):
                if m[0] == r:
                    key_copy(i).wait_send()
            for i, m in enumerate(DK_MSGS):
                if m[0] == r:
                    dk_copy(i).wait_send()
            if r == 0:
                dk_relay.wait_send()
    for t in range(n):
        @pl.when(y >= t)
        def _(t=t):
            for i in range(6):
                dv_copy(t, i).wait_send()

        @pl.when(y > t)
        def _(t=t):
            for c in range(CORES):
                fv_copy(t, c).wait_send()
    oloc.wait()
    qloc.wait()
    orem.wait()
    qrem.wait()


def write_kernel(a, b, c, d, ao, bo, co, do, av, bv, sem):
    parts = 2
    loads = []
    stores = []
    for j, (src, buf, dst) in enumerate(((a, av, ao), (b, bv, bo))):
        for i in range(parts):
            loads.append(pltpu.make_async_copy(src.at[i], buf.at[i], sem.at[j * parts + i]))
            stores.append(pltpu.make_async_copy(buf.at[i], dst.at[i], sem.at[j * parts + i]))
    for cp in loads:
        cp.start()
    co[...] = c[...]
    do[...] = d[...]
    for ld, st in zip(loads, stores):
        ld.wait()
        st.start()
    for st in stores:
        st.wait()


def solution(mesh):
    cp_size = mesh.shape['cp']
    n = SIDE
    assert cp_size == n * n * CORES
    query_spec = P('dp', 'cp', None, None)
    kv_spec = P('dp', 'cp', None)
    pos_spec = P(('dp', 'cp'))

    def per_device(query, key, value, positions, grad_out):
        batch, tokens, heads, head = query.shape
        nrow = tokens * heads
        tab = jnp.stack(rope_tables(positions, head))
        q2 = query.reshape(batch, nrow, head)
        d2 = grad_out.reshape(batch, nrow, head)
        blk = CORES * tokens
        tile = n * blk
        bf16, f32 = jnp.bfloat16, jnp.float32
        V = pltpu.VMEM
        D = pltpu.SemaphoreType.DMA
        scratch = [
            V((CORES, 2, tokens, head // 2), f32),
            V((CORES, nrow, head), bf16),
            V((CORES, nrow, head), bf16),
            V((CORES, tokens, head), bf16),
            V((n, tile, head), bf16),
            V((n, tile, head), bf16),
            V((tile // 2, head), bf16),
            V((n, CORES, nrow, tile), f32),
            V((n, CORES, nrow, tile), f32),
            V((n, CORES, nrow, tile), bf16),
            V((CORES, nrow, 128), f32),
            V((CORES, nrow, 128), f32),
            V((CORES, nrow, 128), f32),
            V((CORES, nrow, 128), f32),
            V((CORES, nrow, head), f32),
            V((CORES, nrow, head), bf16),
            V((CORES, nrow, head), bf16),
            V((n, tile, head), f32),
            V((n, tile, head), f32),
            V((5, tile // 2, head), f32),
            V((n, 6, tokens, head), f32),
            V((n, CORES, tokens, head), f32),
            V((n, CORES, tokens, head), f32),
            V((n, CORES, tokens, head), f32),
            D((4,)), D((2, 5)), D((2, n - 1, CORES)), D((2, n - 1, CORES)), D((2, n, 4)),
            D((len(KEY_MSGS),)), D((4,)),
            D((n, 6)), D((n, 6)), D((len(DK_MSGS) + 1,)), D((5,)),
            D((n, CORES)), D((n, CORES)), D((n, CORES)), D((n, CORES)), D((2, 2)),
        ]
        vmem = pl.BlockSpec(memory_space=pltpu.VMEM)
        hbm = pl.BlockSpec(memory_space=pl.ANY)
        shapes = [jax.ShapeDtypeStruct(a.shape, bf16) for a in (q2, q2, key, value)]
        outs = pl.pallas_call(
            functools.partial(kernel, tokens, heads, head),
            out_shape=shapes,
            in_specs=[vmem, vmem, vmem, hbm, hbm],
            out_specs=[hbm, hbm, vmem, vmem],
            scratch_shapes=scratch,
            compiler_params=pltpu.CompilerParams(collective_id=0, has_side_effects=True,
                                                 vmem_limit_bytes=58 * 1024 * 1024),
        )(tab, key, value, q2, d2)
        outs = pl.pallas_call(
            write_kernel, out_shape=shapes,
            in_specs=[hbm, hbm, vmem, vmem], out_specs=[hbm, hbm, vmem, vmem],
            scratch_shapes=[V(q2.shape, bf16), V(q2.shape, bf16), D((4,))],
        )(*outs)
        out, dq, gk, gv = outs
        return out.reshape(query.shape), dq.reshape(query.shape), gk, gv

    return jax.shard_map(per_device, mesh=mesh, in_specs=(query_spec, kv_spec, kv_spec, pos_spec, query_spec),
                         out_specs=(query_spec, query_spec, kv_spec, kv_spec), check_vma=False)
```

time: 679 us -> 52.6 us (0.08); the launches traced: 668 us -> 52.3 us
  starting transfers between devices: 330 us -> 0 us
  waiting for transfers between devices: 269 us -> 0 us
  Pallas kernels: 0 us -> 50.2 us
  local copies, waits for them, and re-layouts: 43.7 us -> 0.65 us
  matrix products: 13.5 us -> 0 us
  other arithmetic: 8.14 us -> 0.78 us
    ppermute x188 -> x0, starting transfers between devices: 330 us -> none  [the longest x124 308 us: backward_step(): lax.ppermute((key_blk, value_blk, dkey_blk, dvalue_blk), 'cp', shift_pairs)]
    ppermute x188 -> x0, waiting for transfers between devices: 269 us -> none  [the longest x62 195 us: forward_step(): key_blk, value_blk = lax.ppermute((key_blk, value_blk), 'cp', shift_pairs)]
    pallas_call x0 -> x2, Pallas kernels: none -> 50.2 us  [the longest x1 46.4 us: per_device(): pl.pallas_call(functools.partial(kernel, tokens, heads, head), out_shape=...]
    while x188 -> x0, local copies, waits for them, and re-layouts: 40.8 us -> none
    dot_general x13 -> x0, matrix products: 13.5 us -> none  [the longest x3 4.05 us: block_scores(): jnp.einsum('crie,cle->cril', query_rot, key_blk, preferred_element_type=j...]
  transfers between devices with their start and end apart: 188 -> 0, of which waited for: 113 -> 0; matrix products, arithmetic and copies ran while one was open for 0% -> 0% of each run, Pallas kernels for 0% -> 0%
where the time goes in v2:
time: 52.6 us; the launch traced here: 52.3 us
  Pallas kernels  50.2 us (95%)
  other arithmetic  0.78 us (1%)
  local copies, waits for them, and re-layouts  0.65 us (1%)
  between operations  0.65 us (1%)
    pallas_call x1, Pallas kernels, per_device(): pl.pallas_call(functools.partial(kernel, tokens, heads, head), out_shape=...  46.4 us
    pallas_call x1, Pallas kernels, per_device(): pl.pallas_call(write_kernel, out_shape=shapes, in_specs=[hbm, hbm, vmem,...  3.79 us

profile of v2, /device:TPU:97, one launch (start us, length us, event | category | flops | bytes accessed | tf_op | source)
XLA Modules:
  0.0 52.3 jit_solution(17842771909566369587)
XLA Ops:
  0.6 0.0 copy-start
  0.6 0.6 %copy-done = s32[32]{0:T(128)S(1)} copy-done((s32[32]{0:T(128)S(1)}, s32[32]{0:T(128)}, u32[]{:S(2)}) %copy-start) | copy-done | bytes 152
  1.3 0.1 multiply_cosine_fusion
  1.4 0.6 %pad_maximum_fusion.tab_in = f32[2,32,128]{2,1,0:T(8,128)} fusion(f32[1,32,128]{2,1,0:T(8,128)S(1)} %get-tuple-element.21, f32[1,32,128]{2,1,0:T(8,128)S(1)} %get-tuple-element.20), kind=kLoop, calls=%fused_computation | loop fusion | flops 8192 | bytes 65536 | tf_op jit(solution)/shard_map/stack | solution.py:543
  2.1 46.4 %shard_map.84 = (bf16[2,1024,256]{2,1,0:T(8,128)(2,1)}, bf16[2,1024,256]{2,1,0:T(8,128)(2,1)}, bf16[2,32,256]{2,1,0:T(8,128)(2,1)}, bf16[2,32,256]{2,1,0:T(8,128)(2,1)}) custom-call(f32[2,32,128]{2,1,0:T(8,128)} %pad_maximum_fusion.tab_in, bf16[2,32,256]{2,1,0:T(8,128)(2,1)} %key_in.1, bf16[2,32,256]{2,1,0:T(8,128)(2,1)} %val_in.1, ...), custom_call_target="tpu_custom_call" | custom-call | tf_op jit(solution)/shard_map/pallas_call | solution.py:584
  48.5 3.8 %shard_map.85 = (bf16[2,1024,256]{2,1,0:T(8,128)(2,1)}, bf16[2,1024,256]{2,1,0:T(8,128)(2,1)}, bf16[2,32,256]{2,1,0:T(8,128)(2,1)}, bf16[2,32,256]{2,1,0:T(8,128)(2,1)}) custom-call(bf16[2,1024,256]{2,1,0:T(8,128)(2,1)} %get-tuple-element.12.a, bf16[2,1024,256]{2,1,0:T(8,128)(2,1)} %get-tuple-element.13.b, bf16[2,32,256]{2,1,0:T(8,128)(2,1)} %get-tuple-element.14.c, ...), custom_call_target="tpu_custom_call" | custom-call | tf_op jit(solution)/shard_map/pallas_call | solution.py:593
  (2 shorter events, 0.0 us)
Async XLA Ops:
  0.6 0.7 %copy-start = (s32[32]{0:T(128)S(1)}, s32[32]{0:T(128)}, u32[]{:S(2)}) copy-start(s32[32]{0:T(128)} %param.8) | copy-start | bytes 388

commit v3 on v2

--- a/solution.py
+++ b/solution.py
@@ -12,7 +12,6 @@
 CORES = 2
 SIDE = 4
 LOG2E = math.log2(math.e)
-TILE_ORDER = (1, 0, 2, 3)
 
 KEY_MSGS = (
     (0, 0, 0, 1, 0, None), (0, 0, None, 3, 2, None), (0, 0, 1, 1, 1, None),
@@ -22,20 +21,18 @@
 )
 KEY_SLOTS = {(1, 0): (0, 1), (2, 1): (0, 3), (2, 0): (1, 2), (3, 2): (0,), (3, 1): (1, 3), (3, 0): (2,)}
 
-DK_MSGS = (
+DK_HALVES = (
     (3, 1, 0, 2, 0, None), (3, 1, 1, 0, 0, None), (2, 1, 1, 1, 2, None),
     (3, 0, 1, 0, 2, None), (2, 0, 0, 3, 0, None), (2, 0, 1, 1, 0, None), (1, 0, 0, 0, 3, None),
     (3, 2, 0, 2, 1, None), (3, 2, 1, 2, 2, None),
     (3, 0, 0, 0, 1, 0), (2, 1, 0, 1, 1, 0), (1, 0, 1, 0, 4, 0),
 )
-DK_FINAL = ((2, 0, (1,)), (2, 1, (2,)), (1, 0, (1,)), (1, 1, (2, 3)), (0, 0, (1, 3)), (0, 1, (2, 4)))
-
-
-def rope_tables(positions, head):
-    half_dim = head // 2
-    inv_freq = jnp.power(jnp.float32(ROPE_BASE), -2.0 * jnp.arange(half_dim, dtype=jnp.float32) / head)
-    angles = positions.astype(jnp.float32)[..., None] * inv_freq
-    return jnp.cos(angles), jnp.sin(angles)
+DK_MSGS = tuple((r, t, 2 * h + e, dr, 2 * sl + e, None if af is None else 2 * af + e)
+                for r, t, h, dr, sl, af in DK_HALVES for e in range(2))
+DK_RELAY = ((0, 6), (1, 7))
+DK_FINAL = {2: ((1,), (2,)), 1: ((1,), (2, 3)), 0: ((1, 3), (2, 4))}
+DK_QUARTERS = {3: (0, 1, 2, 3), 2: (0, 1, 2, 3), 1: (0, 1, 2, 3), 0: (2, 3, 0, 1)}
+TILE_ORDER = {0: (0,), 1: (0, 1), 2: (0, 1, 2), 3: (1, 0, 2, 3)}
 
 
 def rot_halves(x1, x2, c, s):
@@ -43,9 +40,9 @@
 
 
 def kernel(tokens, heads, head,
-           tab_in, key_in, val_in, q_hbm, do_hbm,
+           pos_ref, freq_hbm, key_hbm, val_hbm, q_hbm, do_hbm,
            out_ref, dq_ref, gk_ref, gv_ref,
-           tabs, qbuf, dobuf, kst, kbuf, vbuf, krel, sbuf, dpbuf, dsbuf, mbuf, lbuf, lse, delta, oacc, obuf, dqbuf,
+           freq_in, ang, key_in, val_in, tab_in, tabs, qbuf, dobuf, kst, kbuf, vbuf, krel, sbuf, dpbuf, dsbuf, mbuf, lbuf, lse, delta, oacc, obuf, dqbuf,
            dk_part, dv_part, rk, rv, vsum, rvy, rkx,
            sem_loc, sem_px, sem_kx, sem_vy, sem_vx, sem_ky_s, sem_ky_r,
            sem_dv_s, sem_dv_r, sem_dk_s, sem_dk_r, sem_fv_s, sem_fv_r, sem_fk_s, sem_fk_r, sem_o):
@@ -80,11 +77,6 @@
 
     def at(i, size):
         return pl.ds(pl.multiple_of(i * size, size), size)
-
-    lq = pltpu.make_async_copy(q_hbm.at[k], qbuf.at[k], sem_loc.at[0])
-    ld = pltpu.make_async_copy(do_hbm.at[k], dobuf.at[k], sem_loc.at[1])
-    lq.start()
-    ld.start()
     bar = pltpu.get_barrier_semaphore()
     peers = [partner]
     for d in range(1, n):
@@ -94,6 +86,23 @@
     for p in peers:
         pl.semaphore_signal(bar, inc=1, device_id={'cp': p}, device_id_type=pl.DeviceIdType.MESH)
 
+    lf = pltpu.make_async_copy(freq_hbm, freq_in, sem_loc.at[4])
+    lk = pltpu.make_async_copy(key_hbm, key_in, sem_loc.at[5])
+    lv = pltpu.make_async_copy(val_hbm, val_in, sem_loc.at[6])
+    lq = pltpu.make_async_copy(q_hbm.at[k], qbuf.at[k], sem_loc.at[0])
+    ld = pltpu.make_async_copy(do_hbm.at[k], dobuf.at[k], sem_loc.at[1])
+    for cp in (lf, lk, lv, lq, ld):
+        cp.start()
+
+    for i in range(tokens):
+        ang[pl.ds(i, 1), :] = jnp.full((1, half), pos_ref[i], jnp.int32).astype(f32)
+    lf.wait()
+    angles = ang[...] * freq_in[...]
+    tab_in[0] = jnp.cos(angles)
+    tab_in[1] = jnp.sin(angles)
+
+    lk.wait()
+    lv.wait()
     for b in range(CORES):
         kf = key_in[b].astype(f32)
         r1, r2 = rot_halves(kf[:, :half], kf[:, half:], tab_in[0], tab_in[1])
@@ -198,6 +207,10 @@
     ld.wait()
     pd.wait_recv()
     vx_relay(0)
+    for d in range(1, n):
+        @pl.when(y - d >= 0)
+        def _(d=d):
+            vx_relay(d)
     vx_copy(0, 2).wait_recv()
     vx_copy(0, 3).wait_recv()
 
@@ -242,10 +255,6 @@
         else:
             lax.fori_loop(0, nrow // rf, rows_body, 0)
     forward_tile(y, True)
-    for d in range(1, n):
-        @pl.when(y - d >= 0)
-        def _(d=d):
-            vx_relay(d)
     for r in range(n - 1):
         @pl.when(y == r)
         def _(r=r):
@@ -304,13 +313,30 @@
             dv_copy(t, i + 2).start()
 
     def dk_copy(i):
-        src, t, hf, dst, slot, after = DK_MSGS[i]
-        return rcopy(dk_part.at[t, pl.ds(hf * ht, ht)], rk.at[slot], sem_dk_s.at[i], sem_dk_r.at[slot], dev(dst, x, k))
-
-    dk_relay = rcopy(rk.at[0], rk.at[3], sem_dk_s.at[len(DK_MSGS)], sem_dk_r.at[3], dev(1, x, k))
+        src, t, qt, dst, slot, after = DK_MSGS[i]
+        return rcopy(dk_part.at[t, pl.ds(qt * blk, blk)], rk.at[slot], sem_dk_s.at[i], sem_dk_r.at[slot], dev(dst, x, k))
+
+    def dk_relay(i):
+        src, dst = DK_RELAY[i]
+        return rcopy(rk.at[src], rk.at[dst], sem_dk_s.at[len(DK_MSGS) + i], sem_dk_r.at[dst], dev(1, x, k))
 
     def dk_wait(slot):
         rcopy(rk.at[slot], rk.at[slot], sem_dk_s.at[0], sem_dk_r.at[slot], partner).wait_recv()
+
+    def dk_combine(e):
+        @pl.when(y == 0)
+        def _():
+            dk_wait(DK_RELAY[e][0])
+            dk_relay(e).start()
+        for r in range(1, n):
+            @pl.when(y == r)
+            def _(r=r):
+                for i, m in enumerate(DK_MSGS):
+                    if m[0] == r and m[5] is not None and m[5] % 2 == e:
+                        dk_wait(m[5])
+                        rows = pl.ds(m[2] * blk, blk)
+                        dk_part[m[1], rows] = dk_part[m[1], rows] + rk[m[5]]
+                        dk_copy(i).start()
 
     def fv_copy(t, c):
         dst = dev(t, x, c)
@@ -328,72 +354,75 @@
         return rcopy(dk_part.at[y, at(x * CORES + other, tokens)], rkx.at[0, k], sem_fk_s.at[0, 0],
                      sem_fk_r.at[0, k if src_core is None else src_core], partner)
 
-    def fk_start():
-        for d in (2, 1, 3):
+    def fk_quarter(xt):
+        @pl.when(x != xt)
+        def _():
+            d = lax.rem(xt - x + n, n)
             for c in range(CORES):
-                fk_copy(d, c).start()
-        fk_own().start()
+                rcopy(dk_part.at[y, pl.ds(xt * blk + c * tokens, tokens)], rkx.at[d, k], sem_fk_s.at[d, c],
+                      sem_fk_r.at[d, k], dev(y, xt, c)).start()
+
+        @pl.when(x == xt)
+        def _():
+            fk_own().start()
 
     rb = 512
 
-    for idx, t in enumerate(TILE_ORDER):
-        @pl.when(y >= t)
-        def _(t=t):
-            dva = None
-            dka = None
-            for s in range(CORES):
-                for i in range(nrow // rb):
-                    rows = pl.ds(i * rb, rb)
-                    ls = lse[s, rows, :]
-                    dl = delta[s, rows, :]
-                    p = jnp.exp2(sbuf[t, s, rows, :] * c2 - jnp.concatenate([ls] * (tile // 128), axis=1))
-                    ds = (p * (dpbuf[t, s, rows, :] - jnp.concatenate([dl] * (tile // 128), axis=1))).astype(bf16)
-                    dsbuf[t, s, rows, :] = ds
-                    a = lax.dot_general(p.astype(bf16), dobuf[s, rows, :], tn, preferred_element_type=f32)
-                    dva = a if dva is None else dva + a
-                    a = lax.dot_general(ds, qbuf[s, rows, :], tn, preferred_element_type=f32)
-                    dka = a if dka is None else dka + a
-            dv_part[t] = dva
-            dk_part[t] = dka * scale
-            for i in (0, 3, 1, 4):
-                dv_copy(t, i).start()
-
-        @pl.when(y < t)
-        def _(t=t):
-            dsbuf[t] = jnp.zeros(dsbuf.shape[1:], bf16)
-            kbuf[t] = jnp.zeros(kbuf.shape[1:], bf16)
-
+    def backward_tile(t):
+        dva = None
+        dka = None
+        for s in range(CORES):
+            for i in range(nrow // rb):
+                rows = pl.ds(i * rb, rb)
+                ls = lse[s, rows, :]
+                dl = delta[s, rows, :]
+                p = jnp.exp2(sbuf[t, s, rows, :] * c2 - jnp.concatenate([ls] * (tile // 128), axis=1))
+                ds = (p * (dpbuf[t, s, rows, :] - jnp.concatenate([dl] * (tile // 128), axis=1))).astype(bf16)
+                dsbuf[t, s, rows, :] = ds
+                a = lax.dot_general(p.astype(bf16), dobuf[s, rows, :], tn, preferred_element_type=f32)
+                dva = a if dva is None else dva + a
+                a = lax.dot_general(ds, qbuf[s, rows, :], tn, preferred_element_type=f32)
+                dka = a if dka is None else dka + a
+        dv_part[t] = dva
+        dk_part[t] = dka * scale
+
+    def dv_order(i):
+        t = i
         for r in range(n):
-            @pl.when(y == r)
-            def _(r=r, t=t):
-                for i, m in enumerate(DK_MSGS):
-                    if m[0] == r and m[1] == t and m[5] is None:
-                        dk_copy(i).start()
-        if idx > 0:
-            tp = TILE_ORDER[idx - 1]
-
-            @pl.when(y >= tp)
-            def _(tp=tp):
-                dv_combine(tp)
-        if t == 2:
-            @pl.when(y == 0)
-            def _():
-                dk_wait(0)
-                dk_relay.start()
-            for r in range(1, n):
-                @pl.when(y == r)
-                def _(r=r):
-                    for i, m in enumerate(DK_MSGS):
-                        if m[0] == r and m[5] is not None:
-                            dk_wait(m[5])
-                            dk_part[m[1], pl.ds(m[2] * ht, ht)] = dk_part[m[1], pl.ds(m[2] * ht, ht)] + rk[m[5]]
-                            dk_copy(i).start()
-    @pl.when(y == n - 1)
-    def _():
-        fk_start()
-        dv_combine(TILE_ORDER[n - 1])
-    for s in range(CORES):
-        def dq_rows(i, carry, s=s):
+            if i < len(TILE_ORDER[r]):
+                t = jnp.where(y == r, TILE_ORDER[r][i], t)
+        return t
+
+    for i in range(n):
+        @pl.when(y >= i)
+        def _(i=i):
+            t = dv_order(i)
+            backward_tile(t)
+            for m in (0, 3, 1, 4):
+                dv_copy(t, m).start()
+            for r in range(n):
+                if i < len(TILE_ORDER[r]):
+                    @pl.when(y == r)
+                    def _(r=r):
+                        for j, m in enumerate(DK_MSGS):
+                            if m[0] == r and m[1] == TILE_ORDER[r][i] and m[5] is None:
+                                dk_copy(j).start()
+
+        @pl.when(y < i)
+        def _(i=i):
+            dsbuf[i] = jnp.zeros(dsbuf.shape[1:], bf16)
+            kbuf[i] = jnp.zeros(kbuf.shape[1:], bf16)
+
+    def dv_turn(i):
+        @pl.when(y >= i)
+        def _():
+            dv_combine(dv_order(i))
+    dv_turn(0)
+    dv_turn(1)
+    dk_combine(0)
+
+    def grad_query_rows(s):
+        def dq_rows(i, carry):
             rows = at(i, rc)
             acc = None
             for t in range(n):
@@ -411,13 +440,24 @@
                 dqbuf[s, orow, half:] = r2.astype(bf16)
             return carry
         lax.fori_loop(0, nrow // rc, dq_rows, 0, unroll=2)
+    grad_query_rows(0)
+    dk_combine(1)
+    dv_turn(2)
+    dv_turn(3)
+
+    @pl.when(y == n - 1)
+    def _():
+        for xt in DK_QUARTERS[n - 1]:
+            fk_quarter(xt)
+    grad_query_rows(1)
     qloc = pltpu.make_async_copy(dqbuf.at[k], dq_ref.at[k], sem_loc.at[3])
     qrem = rcopy(dqbuf.at[other], dq_ref.at[k], sem_o.at[0, 1], sem_o.at[1, 1], partner)
     qloc.start()
     qrem.start()
-    for t in TILE_ORDER:
-        @pl.when(y >= t)
-        def _(t=t):
+    for j in range(n):
+        @pl.when(y >= j)
+        def _(j=j):
+            t = dv_order(j)
             for i in (1, 2, 4, 5):
                 dv_copy(t, i).wait_recv()
             own = at(x * CORES, tokens)
@@ -425,22 +465,22 @@
             vsum[t, 0] = dv_part[t, own] + rv[t, 2] + rv[t, 4]
             vsum[t, 1] = dv_part[t, own2] + rv[t, 1] + rv[t, 5]
 
-        @pl.when(y > t)
-        def _(t=t):
-            for c in range(CORES):
-                fv_copy(t, c).start()
+            @pl.when(y > t)
+            def _():
+                for c in range(CORES):
+                    fv_copy(t, c).start()
     fv_own().start()
     for r in range(n - 1):
         @pl.when(y == r)
         def _(r=r):
-            for row, hf, slots in DK_FINAL:
-                if row == r:
-                    acc = dk_part[r, pl.ds(hf * ht, ht)]
-                    for slot in slots:
-                        dk_wait(slot)
-                        acc = acc + rk[slot]
-                    dk_part[r, pl.ds(hf * ht, ht)] = acc
-            fk_start()
+            for qt in DK_QUARTERS[r]:
+                rows = pl.ds(qt * blk, blk)
+                acc = dk_part[r, rows]
+                for slot in DK_FINAL[r][qt // 2]:
+                    dk_wait(2 * slot + qt % 2)
+                    acc = acc + rk[2 * slot + qt % 2]
+                dk_part[r, rows] = acc
+                fk_quarter(qt)
     def fv_wait(d, b):
         rcopy(rvy.at[d, b], rvy.at[d, b], sem_fv_s.at[0, 0], sem_fv_r.at[d, b], partner).wait_recv()
 
@@ -493,7 +533,8 @@
                 if m[0] == r:
                     dk_copy(i).wait_send()
             if r == 0:
-                dk_relay.wait_send()
+                for i in range(len(DK_RELAY)):
+                    dk_relay(i).wait_send()
     for t in range(n):
         @pl.when(y >= t)
         def _(t=t):
@@ -540,7 +581,7 @@
     def per_device(query, key, value, positions, grad_out):
         batch, tokens, heads, head = query.shape
         nrow = tokens * heads
-        tab = jnp.stack(rope_tables(positions, head))
+        freq = jnp.power(jnp.float32(ROPE_BASE), -2.0 * jnp.arange(head // 2, dtype=jnp.float32) / head)[None, :]
         q2 = query.reshape(batch, nrow, head)
         d2 = grad_out.reshape(batch, nrow, head)
         blk = CORES * tokens
@@ -549,6 +590,11 @@
         V = pltpu.VMEM
         D = pltpu.SemaphoreType.DMA
         scratch = [
+            V((1, head // 2), f32),
+            V((tokens, head // 2), f32),
+            V((batch, tokens, head), bf16),
+            V((batch, tokens, head), bf16),
+            V((2, tokens, head // 2), f32),
             V((CORES, 2, tokens, head // 2), f32),
             V((CORES, nrow, head), bf16),
             V((CORES, nrow, head), bf16),
@@ -568,14 +614,14 @@
             V((CORES, nrow, head), bf16),
             V((n, tile, head), f32),
             V((n, tile, head), f32),
-            V((5, tile // 2, head), f32),
+            V((10, blk, head), f32),
             V((n, 6, tokens, head), f32),
             V((n, CORES, tokens, head), f32),
             V((n, CORES, tokens, head), f32),
             V((n, CORES, tokens, head), f32),
-            D((4,)), D((2, 5)), D((2, n - 1, CORES)), D((2, n - 1, CORES)), D((2, n, 4)),
+            D((7,)), D((2, 5)), D((2, n - 1, CORES)), D((2, n - 1, CORES)), D((2, n, 4)),
             D((len(KEY_MSGS),)), D((4,)),
-            D((n, 6)), D((n, 6)), D((len(DK_MSGS) + 1,)), D((5,)),
+            D((n, 6)), D((n, 6)), D((len(DK_MSGS) + 2,)), D((10,)),
             D((n, CORES)), D((n, CORES)), D((n, CORES)), D((n, CORES)), D((2, 2)),
         ]
         vmem = pl.BlockSpec(memory_space=pltpu.VMEM)
@@ -584,12 +630,12 @@
         outs = pl.pallas_call(
             functools.partial(kernel, tokens, heads, head),
             out_shape=shapes,
-            in_specs=[vmem, vmem, vmem, hbm, hbm],
+            in_specs=[pl.BlockSpec(memory_space=pltpu.SMEM), hbm, hbm, hbm, hbm, hbm],
             out_specs=[hbm, hbm, vmem, vmem],
             scratch_shapes=scratch,
             compiler_params=pltpu.CompilerParams(collective_id=0, has_side_effects=True,
                                                  vmem_limit_bytes=58 * 1024 * 1024),
-        )(tab, key, value, q2, d2)
+        )(positions, freq, key, value, q2, d2)
         outs = pl.pallas_call(
             write_kernel, out_shape=shapes,
             in_specs=[hbm, hbm, vmem, vmem], out_specs=[hbm, hbm, vmem, vmem],

time: 52.6 us -> 47.5 us (0.903)
  Pallas kernels: 50.2 us -> 46.1 us
  local copies, waits for them, and re-layouts: 0.65 us -> 0 us
    pallas_call x1, Pallas kernels: 46.4 us -> 42.3 us  [per_device(): pl.pallas_call(functools.partial(kernel, tokens, heads, head), out_shape=...]
    unnamed x2 -> x0, local copies, waits for them, and re-layouts: 0.65 us -> none
    another operation x1 -> x0, other arithmetic: 0.62 us -> none  [per_device(): tab = jnp.stack(rope_tables(positions, head))]
where the time goes in v3:
time: 47.5 us; the launch traced here: 47.3 us
  Pallas kernels  46.1 us (97%)
  between operations  0.64 us (1%)
  other arithmetic  0.53 us (1%)
    pallas_call x1, Pallas kernels, per_device(): pl.pallas_call(functools.partial(kernel, tokens, heads, head), out_shape=...  42.3 us
    pallas_call x1, Pallas kernels, per_device(): pl.pallas_call(write_kernel, out_shape=shapes, in_specs=[hbm, hbm, vmem,...  3.79 us

profile of v3, /device:TPU:97, one launch (start us, length us, event | category | flops | bytes accessed | tf_op | source)
XLA Modules:
  0.0 47.3 jit_solution(7934668467303541604)
XLA Ops:
  0.6 0.5 %multiply_power_fusion.freq_hbm = f32[1,128]{1,0:T(1,128)} fusion(), kind=kLoop, calls=%fused_computation | loop fusion | flops 128 | bytes 512 | tf_op jit(solution)/shard_map/pow | solution.py:584
  1.2 42.3 %shard_map.84 = (bf16[2,1024,256]{2,1,0:T(8,128)(2,1)}, bf16[2,1024,256]{2,1,0:T(8,128)(2,1)}, bf16[2,32,256]{2,1,0:T(8,128)(2,1)}, bf16[2,32,256]{2,1,0:T(8,128)(2,1)}) custom-call(s32[32]{0:T(128)} %pos_ref.1, f32[1,128]{1,0:T(1,128)} %multiply_power_fusion.freq_hbm, bf16[2,32,256]{2,1,0:T(8,128)(2,1)} %key_hbm.1, bf16[2,32,256]{2,1,0:T(8,128)(2,1)} %val_hbm.1, ...), custom_call_target="tpu_custom_call" | custom-call | tf_op jit(solution)/shard_map/pallas_call | solution.py:630
  43.5 3.8 %shard_map.85 = (bf16[2,1024,256]{2,1,0:T(8,128)(2,1)}, bf16[2,1024,256]{2,1,0:T(8,128)(2,1)}, bf16[2,32,256]{2,1,0:T(8,128)(2,1)}, bf16[2,32,256]{2,1,0:T(8,128)(2,1)}) custom-call(bf16[2,1024,256]{2,1,0:T(8,128)(2,1)} %get-tuple-element.12.a, bf16[2,1024,256]{2,1,0:T(8,128)(2,1)} %get-tuple-element.13.b, bf16[2,32,256]{2,1,0:T(8,128)(2,1)} %get-tuple-element.14.c, ...), custom_call_target="tpu_custom_call" | custom-call | tf_op jit(solution)/shard_map/pallas_call | solution.py:639

commit v4 on v3

--- a/solution.py
+++ b/solution.py
@@ -21,17 +21,20 @@
 )
 KEY_SLOTS = {(1, 0): (0, 1), (2, 1): (0, 3), (2, 0): (1, 2), (3, 2): (0,), (3, 1): (1, 3), (3, 0): (2,)}
 
-DK_HALVES = (
-    (3, 1, 0, 2, 0, None), (3, 1, 1, 0, 0, None), (2, 1, 1, 1, 2, None),
-    (3, 0, 1, 0, 2, None), (2, 0, 0, 3, 0, None), (2, 0, 1, 1, 0, None), (1, 0, 0, 0, 3, None),
-    (3, 2, 0, 2, 1, None), (3, 2, 1, 2, 2, None),
-    (3, 0, 0, 0, 1, 0), (2, 1, 0, 1, 1, 0), (1, 0, 1, 0, 4, 0),
+DK_MSGS = (
+    (3, 1, 0, 2, 0, None, None), (3, 1, 2, 0, 0, None, None), (3, 1, 1, 2, 1, None, None), (3, 1, 3, 0, 1, None, None),
+    (3, 0, 3, 0, 5, None, None),
+    (3, 2, 0, 2, 2, None, None), (3, 2, 1, 2, 3, None, None), (3, 2, 2, 2, 4, None, None), (3, 2, 3, 2, 5, None, None),
+    (2, 0, 3, 1, 0, None, None), (2, 0, 0, 3, 0, None, None), (2, 0, 1, 3, 1, None, None), (2, 0, 2, 3, 2, None, None),
+    (2, 1, 2, 1, 3, None, None), (2, 1, 3, 1, 4, None, None),
+    (1, 0, 0, 0, 6, None, None), (1, 0, 1, 0, 7, None, None), (1, 0, 2, 0, 8, None, None),
+    (3, 0, 0, 0, 2, 0, 0), (3, 0, 1, 0, 3, 1, 0), (3, 0, 2, 0, 4, 2, 1),
+    (2, 1, 0, 1, 1, 0, 0), (2, 1, 1, 1, 2, 1, 1), (1, 0, 3, 0, 9, 0, 0),
 )
-DK_MSGS = tuple((r, t, 2 * h + e, dr, 2 * sl + e, None if af is None else 2 * af + e)
-                for r, t, h, dr, sl, af in DK_HALVES for e in range(2))
-DK_RELAY = ((0, 6), (1, 7))
-DK_FINAL = {2: ((1,), (2,)), 1: ((1,), (2, 3)), 0: ((1, 3), (2, 4))}
-DK_QUARTERS = {3: (0, 1, 2, 3), 2: (0, 1, 2, 3), 1: (0, 1, 2, 3), 0: (2, 3, 0, 1)}
+DK_RELAY = ((0, 5), (1, 6))
+DK_FINAL = {2: ((0, (2,)), (1, (3,)), (2, (4,)), (3, (5,))), 1: ((2, (3, 5)), (3, (4, 6)), (0, (1,)), (1, (2,))),
+            0: ((3, (5, 9)), (0, (2, 6)), (1, (3, 7)), (2, (4, 8)))}
+DV_VIA = ()
 TILE_ORDER = {0: (0,), 1: (0, 1), 2: (0, 1, 2), 3: (1, 0, 2, 3)}
 
 
@@ -43,9 +46,9 @@
            pos_ref, freq_hbm, key_hbm, val_hbm, q_hbm, do_hbm,
            out_ref, dq_ref, gk_ref, gv_ref,
            freq_in, ang, key_in, val_in, tab_in, tabs, qbuf, dobuf, kst, kbuf, vbuf, krel, sbuf, dpbuf, dsbuf, mbuf, lbuf, lse, delta, oacc, obuf, dqbuf,
-           dk_part, dv_part, rk, rv, vsum, rvy, rkx,
+           dk_part, dv_part, rk, rv, vsum, fvb, rvy, rkx,
            sem_loc, sem_px, sem_kx, sem_vy, sem_vx, sem_ky_s, sem_ky_r,
-           sem_dv_s, sem_dv_r, sem_dk_s, sem_dk_r, sem_fv_s, sem_fv_r, sem_fk_s, sem_fk_r, sem_o):
+           sem_dv_s, sem_dv_r, sem_dk_s, sem_dk_r, sem_fv_s, sem_fv_r, sem_fk_s, sem_fk_r, sem_fvb, sem_o):
     n = SIDE
     half = head // 2
     blk = CORES * tokens
@@ -170,9 +173,34 @@
         for i, m in enumerate(KEY_MSGS):
             if m[3] == row and m[4] == slot:
                 key_copy(i).wait_recv()
+
+    def rotate_queries(s):
+        def rotate_rows(tok, carry):
+            rows = at(tok, heads)
+            c = tabs[s, 0, pl.ds(tok, 1), :]
+            sn = tabs[s, 1, pl.ds(tok, 1), :]
+            qf = qbuf[s, rows, :].astype(f32)
+            r1, r2 = rot_halves(qf[:, :half], qf[:, half:], c, sn)
+            qbuf[s, rows, :half] = r1.astype(bf16)
+            qbuf[s, rows, half:] = r2.astype(bf16)
+            return carry
+        lax.fori_loop(0, tokens, rotate_rows, 0, unroll=8)
     pv.wait_recv()
     vx_copy(0, 0).start()
     vx_copy(0, 1).start()
+    lq.wait()
+    rotate_queries(k)
+    for d in range(1, n):
+        @pl.when(y - d >= 0)
+        def _(d=d):
+            for b in range(CORES):
+                vy_copy(d, b, b).wait_recv()
+            vx_copy(d, 0).start()
+            vx_copy(d, 1).start()
+    pt.wait_recv()
+    pq.wait_recv()
+    rotate_queries(other)
+    vx_relay(0)
     pk.wait_recv()
     for d in range(1, n):
         for b in range(CORES):
@@ -183,41 +211,18 @@
             for i, m in enumerate(KEY_MSGS):
                 if m[0] == r and m[5] is None:
                     key_copy(i).start()
-    for d in range(1, n):
-        @pl.when(y - d >= 0)
-        def _(d=d):
-            for b in range(CORES):
-                vy_copy(d, b, b).wait_recv()
-            vx_copy(d, 0).start()
-            vx_copy(d, 1).start()
-    pt.wait_recv()
-    lq.wait()
-    pq.wait_recv()
-    def rotate_rows(tok, carry):
-        for s in range(CORES):
-            rows = at(tok, heads)
-            c = tabs[s, 0, pl.ds(tok, 1), :]
-            sn = tabs[s, 1, pl.ds(tok, 1), :]
-            qf = qbuf[s, rows, :].astype(f32)
-            r1, r2 = rot_halves(qf[:, :half], qf[:, half:], c, sn)
-            qbuf[s, rows, :half] = r1.astype(bf16)
-            qbuf[s, rows, half:] = r2.astype(bf16)
-        return carry
-    lax.fori_loop(0, tokens, rotate_rows, 0, unroll=4)
-    ld.wait()
-    pd.wait_recv()
-    vx_relay(0)
-    for d in range(1, n):
-        @pl.when(y - d >= 0)
-        def _(d=d):
-            vx_relay(d)
-    vx_copy(0, 2).wait_recv()
-    vx_copy(0, 3).wait_recv()
-
     nt = (((1,), (1,)), ((), ()))
     tn = (((0,), (0,)), ((), ()))
 
     rf = 1024
+
+    def first_scores(t):
+        for s in range(CORES):
+            sc = lax.dot_general(qbuf[s], kbuf[t], nt, preferred_element_type=f32)
+            row_tok = (x * CORES + s) * tokens + lax.broadcasted_iota(jnp.int32, sc.shape, 0) // heads
+            sc = jnp.where(lax.broadcasted_iota(jnp.int32, sc.shape, 1) <= row_tok, sc, -jnp.inf)
+            sbuf[t, s] = sc
+            mbuf[s] = jnp.broadcast_to(jnp.max(sc, axis=1, keepdims=True), (nrow, 128))
 
     def forward_tile(t, first):
         kt = kbuf.at[t]
@@ -226,19 +231,16 @@
         def rows_body(i, carry):
             for s in range(CORES):
                 rows = at(i, rf)
-                sc = lax.dot_general(qbuf[s, rows, :], kt[...], nt, preferred_element_type=f32)
                 if first:
-                    row_tok = (x * CORES + s) * tokens + (i * rf + lax.broadcasted_iota(jnp.int32, sc.shape, 0)) // heads
-                    sc = jnp.where(lax.broadcasted_iota(jnp.int32, sc.shape, 1) <= row_tok, sc, -jnp.inf)
-                sbuf[t, s, rows, :] = sc
-                mx = jnp.max(sc, axis=1, keepdims=True)
-                if not first:
+                    sc = sbuf[t, s, rows, :]
+                    mx = mbuf[s, rows, :]
+                else:
+                    sc = lax.dot_general(qbuf[s, rows, :], kt[...], nt, preferred_element_type=f32)
+                    sbuf[t, s, rows, :] = sc
                     old = mbuf[s, rows, :]
-                    mx = jnp.maximum(old, mx)
+                    mx = jnp.maximum(old, jnp.max(sc, axis=1, keepdims=True))
                     fac = jnp.exp2((old - mx) * c2)
-                else:
-                    mx = jnp.broadcast_to(mx, (rf, 128))
-                mbuf[s, rows, :] = mx
+                    mbuf[s, rows, :] = mx
                 mxw = jnp.concatenate([mx] * (tile // 128), axis=1)
                 p = jnp.exp2((sc - mxw) * c2)
                 tot = p[:, :128] + p[:, 128:]
@@ -254,6 +256,15 @@
             rows_body(0, 0)
         else:
             lax.fori_loop(0, nrow // rf, rows_body, 0)
+    first_scores(y)
+    ld.wait()
+    pd.wait_recv()
+    for d in range(1, n):
+        @pl.when(y - d >= 0)
+        def _(d=d):
+            vx_relay(d)
+    vx_copy(0, 2).wait_recv()
+    vx_copy(0, 3).wait_recv()
     forward_tile(y, True)
     for r in range(n - 1):
         @pl.when(y == r)
@@ -282,23 +293,24 @@
                     vx_copy(r - tr, 3).wait_recv()
             forward_tile(t, False)
     rc = 256
-    for s in range(CORES):
-        def out_rows(i, carry, s=s):
+
+    def output_half(s, dst):
+        def out_rows(i, carry):
             rows = at(i, rc)
             tot = jnp.sum(lbuf[s, rows, :], axis=1, keepdims=True)
             inv = 1.0 / tot
             ob = (oacc[s, rows, :] * inv).astype(bf16)
-            obuf[s, rows, :] = ob
+            dst[rows, :] = ob
             dl = jnp.sum(ob.astype(f32) * dobuf[s, rows, :].astype(f32), axis=1, keepdims=True)
             lse[s, rows, :] = mbuf[s, rows, :] * c2 + jnp.broadcast_to(jnp.log2(tot), (rc, 128))
             delta[s, rows, :] = jnp.broadcast_to(dl, (rc, 128))
             return carry
-        lax.fori_loop(0, nrow // rc, out_rows, 0, unroll=2)
-    oloc = pltpu.make_async_copy(obuf.at[k], out_ref.at[k], sem_loc.at[2])
-    orem = rcopy(obuf.at[other], out_ref.at[k], sem_o.at[0, 0], sem_o.at[1, 0], partner)
-    oloc.start()
+        lax.fori_loop(0, nrow // rc, out_rows, 0, unroll=nrow // rc)
+
+    output_half(other, obuf)
+    orem = rcopy(obuf, out_ref.at[k], sem_o.at[0, 0], sem_o.at[1, 0], partner)
     orem.start()
-
+    output_half(k, out_ref.at[k])
     def dv_copy(t, i):
         xt = (xo, xr, xr, xo, xl, xl)[i]
         hf = (0, 1, 0, 1, 0, 1)[i]
@@ -313,7 +325,7 @@
             dv_copy(t, i + 2).start()
 
     def dk_copy(i):
-        src, t, qt, dst, slot, after = DK_MSGS[i]
+        src, t, qt, dst, slot = DK_MSGS[i][:5]
         return rcopy(dk_part.at[t, pl.ds(qt * blk, blk)], rk.at[slot], sem_dk_s.at[i], sem_dk_r.at[slot], dev(dst, x, k))
 
     def dk_relay(i):
@@ -332,7 +344,7 @@
             @pl.when(y == r)
             def _(r=r):
                 for i, m in enumerate(DK_MSGS):
-                    if m[0] == r and m[5] is not None and m[5] % 2 == e:
+                    if m[0] == r and m[6] == e:
                         dk_wait(m[5])
                         rows = pl.ds(m[2] * blk, blk)
                         dk_part[m[1], rows] = dk_part[m[1], rows] + rk[m[5]]
@@ -341,6 +353,10 @@
     def fv_copy(t, c):
         dst = dev(t, x, c)
         return rcopy(vsum.at[t, c], rvy.at[y - t, k], sem_fv_s.at[t, c], sem_fv_r.at[y - t, k], dst)
+
+    def fv_via(row):
+        t = {2: 1, 1: 0}[row]
+        return rcopy(vsum.at[t], fvb, sem_fvb.at[0], sem_fvb.at[1], dev(row, x, k))
 
     def fv_own():
         return rcopy(vsum.at[y, other], rvy.at[0, k], sem_fv_s.at[y, other], sem_fv_r.at[0, k], partner)
@@ -393,12 +409,17 @@
                 t = jnp.where(y == r, TILE_ORDER[r][i], t)
         return t
 
+    def dv_turn(i):
+        @pl.when(y >= i)
+        def _():
+            dv_combine(dv_order(i))
+
     for i in range(n):
         @pl.when(y >= i)
         def _(i=i):
             t = dv_order(i)
             backward_tile(t)
-            for m in (0, 3, 1, 4):
+            for m in ((0, 3, 1, 4) if i < 2 else (0, 3)):
                 dv_copy(t, m).start()
             for r in range(n):
                 if i < len(TILE_ORDER[r]):
@@ -413,15 +434,17 @@
             dsbuf[i] = jnp.zeros(dsbuf.shape[1:], bf16)
             kbuf[i] = jnp.zeros(kbuf.shape[1:], bf16)
 
-    def dv_turn(i):
-        @pl.when(y >= i)
-        def _():
-            dv_combine(dv_order(i))
-    dv_turn(0)
-    dv_turn(1)
+        if i >= 2:
+            dv_turn(i - 2)
+
+            @pl.when(y >= i)
+            def _(i=i):
+                t = dv_order(i)
+                for m in (1, 4):
+                    dv_copy(t, m).start()
     dk_combine(0)
 
-    def grad_query_rows(s):
+    def grad_query_half(s, dst):
         def dq_rows(i, carry):
             rows = at(i, rc)
             acc = None
@@ -436,58 +459,86 @@
                 g = acc[j * heads:(j + 1) * heads]
                 r1, r2 = rot_halves(g[:, :half], g[:, half:], c, -sn)
                 orow = at(tok, heads)
-                dqbuf[s, orow, :half] = r1.astype(bf16)
-                dqbuf[s, orow, half:] = r2.astype(bf16)
+                dst[orow, :half] = r1.astype(bf16)
+                dst[orow, half:] = r2.astype(bf16)
             return carry
         lax.fori_loop(0, nrow // rc, dq_rows, 0, unroll=2)
-    grad_query_rows(0)
+    grad_query_half(other, dqbuf)
+    qrem = rcopy(dqbuf, dq_ref.at[k], sem_o.at[0, 1], sem_o.at[1, 1], partner)
+    qrem.start()
     dk_combine(1)
-    dv_turn(2)
-    dv_turn(3)
-
-    @pl.when(y == n - 1)
-    def _():
-        for xt in DK_QUARTERS[n - 1]:
-            fk_quarter(xt)
-    grad_query_rows(1)
-    qloc = pltpu.make_async_copy(dqbuf.at[k], dq_ref.at[k], sem_loc.at[3])
-    qrem = rcopy(dqbuf.at[other], dq_ref.at[k], sem_o.at[0, 1], sem_o.at[1, 1], partner)
-    qloc.start()
-    qrem.start()
-    for j in range(n):
+
+    def dv_total(j):
         @pl.when(y >= j)
-        def _(j=j):
+        def _():
             t = dv_order(j)
             for i in (1, 2, 4, 5):
                 dv_copy(t, i).wait_recv()
-            own = at(x * CORES, tokens)
-            own2 = at(x * CORES + 1, tokens)
-            vsum[t, 0] = dv_part[t, own] + rv[t, 2] + rv[t, 4]
-            vsum[t, 1] = dv_part[t, own2] + rv[t, 1] + rv[t, 5]
-
-            @pl.when(y > t)
+            vsum[t, 0] = dv_part[t, at(x * CORES, tokens)] + rv[t, 2] + rv[t, 4]
+            vsum[t, 1] = dv_part[t, at(x * CORES + 1, tokens)] + rv[t, 1] + rv[t, 5]
+            for r, t_on, via in DV_VIA:
+                @pl.when((y == r) & (t == t_on))
+                def _(via=via):
+                    fv_via(via).start()
+
+            direct = y > t
+            for r, t_on, via in DV_VIA:
+                direct = direct & ((y != r) | (t != t_on)) & ((y != via) | (t != t_on))
+
+            @pl.when(direct)
             def _():
                 for c in range(CORES):
                     fv_copy(t, c).start()
+
+    def dv_via(r, t_on):
+        @pl.when(y == r)
+        def _():
+            fv_via(r).wait_recv()
+            vsum[t_on] = vsum[t_on] + fvb[...]
+            for c in range(CORES):
+                fv_copy(t_on, c).start()
+
+    def dk_final(part):
+        for r in range(n - 1):
+            @pl.when(y == r)
+            def _(r=r):
+                for qt, slots in DK_FINAL[r][2 * part:2 * part + 2]:
+                    rows = pl.ds(qt * blk, blk)
+                    acc = dk_part[r, rows]
+                    for slot in slots:
+                        dk_wait(slot)
+                        acc = acc + rk[slot]
+                    dk_part[r, rows] = acc
+                    fk_quarter(qt)
+    dv_turn(2)
+    dv_total(0)
+    dv_turn(3)
+
+    @pl.when(y == n - 1)
+    def _():
+        for xt in range(n):
+            fk_quarter(xt)
+    dv_total(1)
+    grad_query_half(k, dq_ref.at[k])
+    dv_total(2)
+    dv_total(3)
     fv_own().start()
-    for r in range(n - 1):
-        @pl.when(y == r)
-        def _(r=r):
-            for qt in DK_QUARTERS[r]:
-                rows = pl.ds(qt * blk, blk)
-                acc = dk_part[r, rows]
-                for slot in DK_FINAL[r][qt // 2]:
-                    dk_wait(2 * slot + qt % 2)
-                    acc = acc + rk[2 * slot + qt % 2]
-                dk_part[r, rows] = acc
-                fk_quarter(qt)
+    dk_final(0)
+    for r, t_on, via in DV_VIA:
+        dv_via(via, t_on)
+    dk_final(1)
     def fv_wait(d, b):
         rcopy(rvy.at[d, b], rvy.at[d, b], sem_fv_s.at[0, 0], sem_fv_r.at[d, b], partner).wait_recv()
 
     fv_wait(0, other)
     rvy[0, k] = vsum[y, k]
     for d in range(1, n):
-        @pl.when(y + d < n)
+        expect = y + d < n
+        for r, t_on, via in DV_VIA:
+            if r - t_on == d:
+                expect = expect & (y != t_on)
+
+        @pl.when(expect)
         def _(d=d):
             for b in range(CORES):
                 fv_wait(d, b)
@@ -541,33 +592,29 @@
             for i in range(6):
                 dv_copy(t, i).wait_send()
 
-        @pl.when(y > t)
+        sent = y > t
+        for r, t_on, via in DV_VIA:
+            if t == t_on:
+                sent = sent & (y != r)
+
+        @pl.when(sent)
         def _(t=t):
             for c in range(CORES):
                 fv_copy(t, c).wait_send()
-    oloc.wait()
-    qloc.wait()
+    for r, t_on, via in DV_VIA:
+        @pl.when(y == r)
+        def _(via=via):
+            fv_via(via).wait_send()
     orem.wait()
     qrem.wait()
 
 
-def write_kernel(a, b, c, d, ao, bo, co, do, av, bv, sem):
-    parts = 2
-    loads = []
-    stores = []
-    for j, (src, buf, dst) in enumerate(((a, av, ao), (b, bv, bo))):
-        for i in range(parts):
-            loads.append(pltpu.make_async_copy(src.at[i], buf.at[i], sem.at[j * parts + i]))
-            stores.append(pltpu.make_async_copy(buf.at[i], dst.at[i], sem.at[j * parts + i]))
-    for cp in loads:
+def write_kernel(a, b, c, d, ao, bo, co, do, sem):
+    cps = [pltpu.make_async_copy(s, t, sem.at[i]) for i, (s, t) in enumerate(((a, ao), (b, bo), (c, co), (d, do)))]
+    for cp in cps:
         cp.start()
-    co[...] = c[...]
-    do[...] = d[...]
-    for ld, st in zip(loads, stores):
-        ld.wait()
-        st.start()
-    for st in stores:
-        st.wait()
+    for cp in cps:
+        cp.wait()
 
 
 def solution(mesh):
@@ -610,37 +657,38 @@
             V((CORES, nrow, 128), f32),
             V((CORES, nrow, 128), f32),
             V((CORES, nrow, head), f32),
-            V((CORES, nrow, head), bf16),
-            V((CORES, nrow, head), bf16),
+            V((nrow, head), bf16),
+            V((nrow, head), bf16),
             V((n, tile, head), f32),
             V((n, tile, head), f32),
             V((10, blk, head), f32),
             V((n, 6, tokens, head), f32),
             V((n, CORES, tokens, head), f32),
+            V((CORES, tokens, head), f32),
             V((n, CORES, tokens, head), f32),
             V((n, CORES, tokens, head), f32),
             D((7,)), D((2, 5)), D((2, n - 1, CORES)), D((2, n - 1, CORES)), D((2, n, 4)),
             D((len(KEY_MSGS),)), D((4,)),
             D((n, 6)), D((n, 6)), D((len(DK_MSGS) + 2,)), D((10,)),
-            D((n, CORES)), D((n, CORES)), D((n, CORES)), D((n, CORES)), D((2, 2)),
+            D((n, CORES)), D((n, CORES)), D((n, CORES)), D((n, CORES)), D((2,)), D((2, 2)),
         ]
         vmem = pl.BlockSpec(memory_space=pltpu.VMEM)
         hbm = pl.BlockSpec(memory_space=pl.ANY)
         shapes = [jax.ShapeDtypeStruct(a.shape, bf16) for a in (q2, q2, key, value)]
         outs = pl.pallas_call(
             functools.partial(kernel, tokens, heads, head),
-            out_shape=shapes,
+            out_shape=[pltpu.VMEM(a.shape, bf16) for a in (q2, q2, key, value)],
             in_specs=[pl.BlockSpec(memory_space=pltpu.SMEM), hbm, hbm, hbm, hbm, hbm],
-            out_specs=[hbm, hbm, vmem, vmem],
+            out_specs=[vmem, vmem, vmem, vmem],
             scratch_shapes=scratch,
             compiler_params=pltpu.CompilerParams(collective_id=0, has_side_effects=True,
                                                  vmem_limit_bytes=58 * 1024 * 1024),
         )(positions, freq, key, value, q2, d2)
         outs = pl.pallas_call(
             write_kernel, out_shape=shapes,
-            in_specs=[hbm, hbm, vmem, vmem], out_specs=[hbm, hbm, vmem, vmem],
-            scratch_shapes=[V(q2.shape, bf16), V(q2.shape, bf16), D((4,))],
-        )(*outs)
+            in_specs=[vmem, vmem, vmem, vmem], out_specs=[hbm, hbm, hbm, hbm],
+            scratch_shapes=[D((4,))],
+        )(*[pltpu.with_memory_space_constraint(o, V) for o in outs])
         out, dq, gk, gv = outs
         return out.reshape(query.shape), dq.reshape(query.shape), gk, gv
 

time: 47.5 us -> 42.8 us (0.901)
  Pallas kernels: 46.1 us -> 41.3 us
    pallas_call x1, Pallas kernels: 3.79 us -> 1.36 us  [per_device(): pl.pallas_call(write_kernel, out_shape=shapes, in_specs=[vmem, vmem, vmem...]
    pallas_call x1, Pallas kernels: 42.3 us -> 40 us  [per_device(): pl.pallas_call(functools.partial(kernel, tokens, heads, head), out_shape=...]
where the time goes in v4:
time: 42.8 us; the launch traced here: 42.7 us
  Pallas kernels  41.3 us (96%)
  between operations  0.8 us (2%)
  other arithmetic  0.53 us (1%)
    pallas_call x1, Pallas kernels, per_device(): pl.pallas_call(functools.partial(kernel, tokens, heads, head), out_shape=...  40 us
    pallas_call x1, Pallas kernels, per_device(): pl.pallas_call(write_kernel, out_shape=shapes, in_specs=[vmem, vmem, vmem...  1.36 us

profile of v4, /device:TPU:97, one launch (start us, length us, event | category | flops | bytes accessed | tf_op | source)
XLA Modules:
  0.0 42.7 jit_solution(18030319450312973120)
XLA Ops:
  0.6 0.5 %multiply_power_fusion.freq_hbm = f32[1,128]{1,0:T(1,128)} fusion(), kind=kLoop, calls=%fused_computation | loop fusion | flops 128 | bytes 512 | tf_op jit(solution)/shard_map/pow | solution.py:631
  1.2 40.0 %shard_map.84 = (bf16[2,1024,256]{2,1,0:T(8,128)(2,1)S(1)}, bf16[2,1024,256]{2,1,0:T(8,128)(2,1)S(1)}, bf16[2,32,256]{2,1,0:T(8,128)(2,1)S(1)}, bf16[2,32,256]{2,1,0:T(8,128)(2,1)S(1)}) custom-call(s32[32]{0:T(128)} %pos_ref.1, f32[1,128]{1,0:T(1,128)} %multiply_power_fusion.freq_hbm, bf16[2,32,256]{2,1,0:T(8,128)(2,1)} %key_hbm.1, ...), custom_call_target="tpu_custom_call" | custom-call | tf_op jit(solution)/shard_map/pallas_call | solution.py:678
  41.1 1.4 %shard_map.85 = (bf16[2,1024,256]{2,1,0:T(8,128)(2,1)}, bf16[2,1024,256]{2,1,0:T(8,128)(2,1)}, bf16[2,32,256]{2,1,0:T(8,128)(2,1)}, bf16[2,32,256]{2,1,0:T(8,128)(2,1)}) custom-call(bf16[2,1024,256]{2,1,0:T(8,128)(2,1)S(1)} %get-tuple-element.12.a, bf16[2,1024,256]{2,1,0:T(8,128)(2,1)S(1)} %get-tuple-element.13.b, ...), custom_call_target="tpu_custom_call" | custom-call | tf_op jit(solution)/shard_map/pallas_call | solution.py:687

commit v5 on v4

--- a/solution.py
+++ b/solution.py
@@ -43,9 +43,9 @@
 
 
 def kernel(tokens, heads, head,
-           pos_ref, freq_hbm, key_hbm, val_hbm, q_hbm, do_hbm,
+           pos_hbm, key_hbm, val_hbm, q_hbm, do_hbm,
            out_ref, dq_ref, gk_ref, gv_ref,
-           freq_in, ang, key_in, val_in, tab_in, tabs, qbuf, dobuf, kst, kbuf, vbuf, krel, sbuf, dpbuf, dsbuf, mbuf, lbuf, lse, delta, oacc, obuf, dqbuf,
+           pos_ref, ang, key_in, val_in, tab_in, tabs, qbuf, dobuf, kst, kbuf, vbuf, krel, sbuf, dpbuf, dsbuf, mbuf, lbuf, lse, delta, oacc, obuf, dqbuf,
            dk_part, dv_part, rk, rv, vsum, fvb, rvy, rkx,
            sem_loc, sem_px, sem_kx, sem_vy, sem_vx, sem_ky_s, sem_ky_r,
            sem_dv_s, sem_dv_r, sem_dk_s, sem_dk_r, sem_fv_s, sem_fv_r, sem_fk_s, sem_fk_r, sem_fvb, sem_o):
@@ -89,7 +89,7 @@
     for p in peers:
         pl.semaphore_signal(bar, inc=1, device_id={'cp': p}, device_id_type=pl.DeviceIdType.MESH)
 
-    lf = pltpu.make_async_copy(freq_hbm, freq_in, sem_loc.at[4])
+    lf = pltpu.make_async_copy(pos_hbm, pos_ref, sem_loc.at[4])
     lk = pltpu.make_async_copy(key_hbm, key_in, sem_loc.at[5])
     lv = pltpu.make_async_copy(val_hbm, val_in, sem_loc.at[6])
     lq = pltpu.make_async_copy(q_hbm.at[k], qbuf.at[k], sem_loc.at[0])
@@ -97,10 +97,12 @@
     for cp in (lf, lk, lv, lq, ld):
         cp.start()
 
+    pair = lax.broadcasted_iota(jnp.int32, (1, half), 1).astype(f32)
+    freq = jnp.exp2(pair * (-2.0 * math.log2(ROPE_BASE) / head))
+    lf.wait()
     for i in range(tokens):
         ang[pl.ds(i, 1), :] = jnp.full((1, half), pos_ref[i], jnp.int32).astype(f32)
-    lf.wait()
-    angles = ang[...] * freq_in[...]
+    angles = ang[...] * freq
     tab_in[0] = jnp.cos(angles)
     tab_in[1] = jnp.sin(angles)
 
@@ -294,9 +296,9 @@
             forward_tile(t, False)
     rc = 256
 
-    def output_half(s, dst):
-        def out_rows(i, carry):
-            rows = at(i, rc)
+    for i in range(nrow // rc):
+        for s, dst in ((other, obuf), (k, out_ref.at[k])):
+            rows = pl.ds(i * rc, rc)
             tot = jnp.sum(lbuf[s, rows, :], axis=1, keepdims=True)
             inv = 1.0 / tot
             ob = (oacc[s, rows, :] * inv).astype(bf16)
@@ -304,13 +306,7 @@
             dl = jnp.sum(ob.astype(f32) * dobuf[s, rows, :].astype(f32), axis=1, keepdims=True)
             lse[s, rows, :] = mbuf[s, rows, :] * c2 + jnp.broadcast_to(jnp.log2(tot), (rc, 128))
             delta[s, rows, :] = jnp.broadcast_to(dl, (rc, 128))
-            return carry
-        lax.fori_loop(0, nrow // rc, out_rows, 0, unroll=nrow // rc)
-
-    output_half(other, obuf)
     orem = rcopy(obuf, out_ref.at[k], sem_o.at[0, 0], sem_o.at[1, 0], partner)
-    orem.start()
-    output_half(k, out_ref.at[k])
     def dv_copy(t, i):
         xt = (xo, xr, xr, xo, xl, xl)[i]
         hf = (0, 1, 0, 1, 0, 1)[i]
@@ -415,10 +411,14 @@
             dv_combine(dv_order(i))
 
     for i in range(n):
+        if i == 0:
+            backward_tile(dv_order(0))
+
         @pl.when(y >= i)
         def _(i=i):
             t = dv_order(i)
-            backward_tile(t)
+            if i > 0:
+                backward_tile(t)
             for m in ((0, 3, 1, 4) if i < 2 else (0, 3)):
                 dv_copy(t, m).start()
             for r in range(n):
@@ -434,14 +434,17 @@
             dsbuf[i] = jnp.zeros(dsbuf.shape[1:], bf16)
             kbuf[i] = jnp.zeros(kbuf.shape[1:], bf16)
 
+        if i == 0:
+            orem.start()
         if i >= 2:
             dv_turn(i - 2)
-
-            @pl.when(y >= i)
-            def _(i=i):
-                t = dv_order(i)
-                for m in (1, 4):
-                    dv_copy(t, m).start()
+        if i == n - 1:
+            for j in range(2, n):
+                @pl.when(y >= j)
+                def _(j=j):
+                    t = dv_order(j)
+                    for m in (1, 4):
+                        dv_copy(t, m).start()
     dk_combine(0)
 
     def grad_query_half(s, dst):
@@ -610,7 +613,16 @@
 
 
 def write_kernel(a, b, c, d, ao, bo, co, do, sem):
-    cps = [pltpu.make_async_copy(s, t, sem.at[i]) for i, (s, t) in enumerate(((a, ao), (b, bo), (c, co), (d, do)))]
+    pieces = 1
+    cps = []
+    for src, dst in ((a, ao), (b, bo)):
+        rows = src.shape[1] // pieces
+        for e in range(src.shape[0]):
+            for i in range(pieces):
+                at = (e, pl.ds(i * rows, rows))
+                cps.append(pltpu.make_async_copy(src.at[at], dst.at[at], sem.at[len(cps)]))
+    for src, dst in ((c, co), (d, do)):
+        cps.append(pltpu.make_async_copy(src, dst, sem.at[len(cps)]))
     for cp in cps:
         cp.start()
     for cp in cps:
@@ -628,7 +640,6 @@
     def per_device(query, key, value, positions, grad_out):
         batch, tokens, heads, head = query.shape
         nrow = tokens * heads
-        freq = jnp.power(jnp.float32(ROPE_BASE), -2.0 * jnp.arange(head // 2, dtype=jnp.float32) / head)[None, :]
         q2 = query.reshape(batch, nrow, head)
         d2 = grad_out.reshape(batch, nrow, head)
         blk = CORES * tokens
@@ -637,7 +648,7 @@
         V = pltpu.VMEM
         D = pltpu.SemaphoreType.DMA
         scratch = [
-            V((1, head // 2), f32),
+            pltpu.SMEM((tokens,), jnp.int32),
             V((tokens, head // 2), f32),
             V((batch, tokens, head), bf16),
             V((batch, tokens, head), bf16),
@@ -678,16 +689,16 @@
         outs = pl.pallas_call(
             functools.partial(kernel, tokens, heads, head),
             out_shape=[pltpu.VMEM(a.shape, bf16) for a in (q2, q2, key, value)],
-            in_specs=[pl.BlockSpec(memory_space=pltpu.SMEM), hbm, hbm, hbm, hbm, hbm],
+            in_specs=[hbm] * 5,
             out_specs=[vmem, vmem, vmem, vmem],
             scratch_shapes=scratch,
             compiler_params=pltpu.CompilerParams(collective_id=0, has_side_effects=True,
                                                  vmem_limit_bytes=58 * 1024 * 1024),
-        )(positions, freq, key, value, q2, d2)
+        )(positions, key, value, q2, d2)
         outs = pl.pallas_call(
             write_kernel, out_shape=shapes,
             in_specs=[vmem, vmem, vmem, vmem], out_specs=[hbm, hbm, hbm, hbm],
-            scratch_shapes=[D((4,))],
+            scratch_shapes=[D((4 * 1 + 2,))],
         )(*[pltpu.with_memory_space_constraint(o, V) for o in outs])
         out, dq, gk, gv = outs
         return out.reshape(query.shape), dq.reshape(query.shape), gk, gv

time: 42.8 us -> 41.4 us (0.967)
  Pallas kernels: 41.3 us -> 40.5 us
  other arithmetic: 0.53 us -> 0 us
    pallas_call x1, Pallas kernels: 40 us -> 39.1 us  [per_device(): pl.pallas_call(functools.partial(kernel, tokens, heads, head), out_shape=...]
    pow x1 -> x0, other arithmetic: 0.53 us -> none  [per_device(): jnp.power(jnp.float32(ROPE_BASE), -2.0 * jnp.arange(head // 2, dtype=jnp....]
where the time goes in v5:
time: 41.4 us; the launch traced here: 41.3 us
  Pallas kernels  40.5 us (98%)
  between operations  0.8 us (2%)
    pallas_call x1, Pallas kernels, per_device(): pl.pallas_call(functools.partial(kernel, tokens, heads, head), out_shape=...  39.1 us
    pallas_call x1, Pallas kernels, per_device(): pl.pallas_call(write_kernel, out_shape=shapes, in_specs=[vmem, vmem, vmem...  1.37 us

profile of v5, /device:TPU:97, one launch (start us, length us, event | category | flops | bytes accessed | tf_op | source)
XLA Modules:
  0.0 41.3 jit_solution(15524420570404856592)
XLA Ops:
  0.6 39.1 %shard_map.84 = (bf16[2,1024,256]{2,1,0:T(8,128)(2,1)S(1)}, bf16[2,1024,256]{2,1,0:T(8,128)(2,1)S(1)}, bf16[2,32,256]{2,1,0:T(8,128)(2,1)S(1)}, bf16[2,32,256]{2,1,0:T(8,128)(2,1)S(1)}) custom-call(s32[32]{0:T(128)} %pos_hbm.1, bf16[2,32,256]{2,1,0:T(8,128)(2,1)} %key_hbm.1, bf16[2,32,256]{2,1,0:T(8,128)(2,1)} %val_hbm.1, bf16[2,1024,256]{2,1,0:T(8,128)(2,1)} %bitcast.4, ...), custom_call_target="tpu_custom_call" | custom-call | tf_op jit(solution)/shard_map/pallas_call | solution.py:689
  39.7 1.4 %shard_map.85 = (bf16[2,1024,256]{2,1,0:T(8,128)(2,1)}, bf16[2,1024,256]{2,1,0:T(8,128)(2,1)}, bf16[2,32,256]{2,1,0:T(8,128)(2,1)}, bf16[2,32,256]{2,1,0:T(8,128)(2,1)}) custom-call(bf16[2,1024,256]{2,1,0:T(8,128)(2,1)S(1)} %get-tuple-element.12.a, bf16[2,1024,256]{2,1,0:T(8,128)(2,1)S(1)} %get-tuple-element.13.b, ...), custom_call_target="tpu_custom_call" | custom-call | tf_op jit(solution)/shard_map/pallas_call | solution.py:698

commit v6 on v5

--- a/solution.py
+++ b/solution.py
@@ -22,17 +22,17 @@
 KEY_SLOTS = {(1, 0): (0, 1), (2, 1): (0, 3), (2, 0): (1, 2), (3, 2): (0,), (3, 1): (1, 3), (3, 0): (2,)}
 
 DK_MSGS = (
-    (3, 1, 0, 2, 0, None, None), (3, 1, 2, 0, 0, None, None), (3, 1, 1, 2, 1, None, None), (3, 1, 3, 0, 1, None, None),
+    (3, 1, 0, 2, 0, None, None), (3, 1, 2, 0, 0, None, None), (3, 1, 1, 2, 1, None, None), (3, 1, 3, 2, 6, None, None),
     (3, 0, 3, 0, 5, None, None),
     (3, 2, 0, 2, 2, None, None), (3, 2, 1, 2, 3, None, None), (3, 2, 2, 2, 4, None, None), (3, 2, 3, 2, 5, None, None),
     (2, 0, 3, 1, 0, None, None), (2, 0, 0, 3, 0, None, None), (2, 0, 1, 3, 1, None, None), (2, 0, 2, 3, 2, None, None),
-    (2, 1, 2, 1, 3, None, None), (2, 1, 3, 1, 4, None, None),
+    (2, 1, 2, 1, 3, None, None),
     (1, 0, 0, 0, 6, None, None), (1, 0, 1, 0, 7, None, None), (1, 0, 2, 0, 8, None, None),
     (3, 0, 0, 0, 2, 0, 0), (3, 0, 1, 0, 3, 1, 0), (3, 0, 2, 0, 4, 2, 1),
-    (2, 1, 0, 1, 1, 0, 0), (2, 1, 1, 1, 2, 1, 1), (1, 0, 3, 0, 9, 0, 0),
+    (2, 1, 0, 1, 1, 0, 0), (2, 1, 1, 1, 2, 1, 1), (2, 1, 3, 1, 4, 6, 1), (1, 0, 3, 0, 9, 0, 0),
 )
-DK_RELAY = ((0, 5), (1, 6))
-DK_FINAL = {2: ((0, (2,)), (1, (3,)), (2, (4,)), (3, (5,))), 1: ((2, (3, 5)), (3, (4, 6)), (0, (1,)), (1, (2,))),
+DK_RELAY = ((0, 5),)
+DK_FINAL = {2: ((0, (2,)), (1, (3,)), (2, (4,)), (3, (5,))), 1: ((2, (3, 5)), (0, (1,)), (1, (2,)), (3, (4,))),
             0: ((3, (5, 9)), (0, (2, 6)), (1, (3, 7)), (2, (4, 8)))}
 DV_VIA = ()
 TILE_ORDER = {0: (0,), 1: (0, 1), 2: (0, 1, 2), 3: (1, 0, 2, 3)}
@@ -331,12 +331,15 @@
     def dk_wait(slot):
         rcopy(rk.at[slot], rk.at[slot], sem_dk_s.at[0], sem_dk_r.at[slot], partner).wait_recv()
 
-    def dk_combine(e):
-        @pl.when(y == 0)
-        def _():
-            dk_wait(DK_RELAY[e][0])
-            dk_relay(e).start()
+    def dk_combine(e, rows_here):
+        if 0 in rows_here and e < len(DK_RELAY):
+            @pl.when(y == 0)
+            def _():
+                dk_wait(DK_RELAY[e][0])
+                dk_relay(e).start()
         for r in range(1, n):
+            if r not in rows_here:
+                continue
             @pl.when(y == r)
             def _(r=r):
                 for i, m in enumerate(DK_MSGS):
@@ -437,6 +440,8 @@
         if i == 0:
             orem.start()
         if i >= 2:
+            if i == n - 1:
+                dk_combine(0, (3,))
             dv_turn(i - 2)
         if i == n - 1:
             for j in range(2, n):
@@ -445,7 +450,7 @@
                     t = dv_order(j)
                     for m in (1, 4):
                         dv_copy(t, m).start()
-    dk_combine(0)
+    dk_combine(0, (0, 1, 2))
 
     def grad_query_half(s, dst):
         def dq_rows(i, carry):
@@ -469,7 +474,7 @@
     grad_query_half(other, dqbuf)
     qrem = rcopy(dqbuf, dq_ref.at[k], sem_o.at[0, 1], sem_o.at[1, 1], partner)
     qrem.start()
-    dk_combine(1)
+    dk_combine(1, (0, 1, 2, 3))
 
     def dv_total(j):
         @pl.when(y >= j)

time: 41.4 us -> 40.5 us (0.978)
  Pallas kernels: 40.5 us -> 39.6 us
    pallas_call x1, Pallas kernels: 39.1 us -> 38.3 us  [per_device(): pl.pallas_call(functools.partial(kernel, tokens, heads, head), out_shape=...]
where the time goes in v6:
time: 40.5 us; the launch traced here: 40.4 us
  Pallas kernels  39.6 us (98%)
  between operations  0.8 us (2%)
    pallas_call x1, Pallas kernels, per_device(): pl.pallas_call(functools.partial(kernel, tokens, heads, head), out_shape=...  38.3 us
    pallas_call x1, Pallas kernels, per_device(): pl.pallas_call(write_kernel, out_shape=shapes, in_specs=[vmem, vmem, vmem...  1.37 us

profile of v6, /device:TPU:97, one launch (start us, length us, event | category | flops | bytes accessed | tf_op | source)
XLA Modules:
  0.0 40.4 jit_solution(10106487740740695135)
XLA Ops:
  0.6 38.3 %shard_map.84 = (bf16[2,1024,256]{2,1,0:T(8,128)(2,1)S(1)}, bf16[2,1024,256]{2,1,0:T(8,128)(2,1)S(1)}, bf16[2,32,256]{2,1,0:T(8,128)(2,1)S(1)}, bf16[2,32,256]{2,1,0:T(8,128)(2,1)S(1)}) custom-call(s32[32]{0:T(128)} %pos_hbm.1, bf16[2,32,256]{2,1,0:T(8,128)(2,1)} %key_hbm.1, bf16[2,32,256]{2,1,0:T(8,128)(2,1)} %val_hbm.1, bf16[2,1024,256]{2,1,0:T(8,128)(2,1)} %bitcast.4, ...), custom_call_target="tpu_custom_call" | custom-call | tf_op jit(solution)/shard_map/pallas_call | solution.py:694
  38.9 1.4 %shard_map.85 = (bf16[2,1024,256]{2,1,0:T(8,128)(2,1)}, bf16[2,1024,256]{2,1,0:T(8,128)(2,1)}, bf16[2,32,256]{2,1,0:T(8,128)(2,1)}, bf16[2,32,256]{2,1,0:T(8,128)(2,1)}) custom-call(bf16[2,1024,256]{2,1,0:T(8,128)(2,1)S(1)} %get-tuple-element.12.a, bf16[2,1024,256]{2,1,0:T(8,128)(2,1)S(1)} %get-tuple-element.13.b, ...), custom_call_target="tpu_custom_call" | custom-call | tf_op jit(solution)/shard_map/pallas_call | solution.py:703

commit v7 on v6

--- a/solution.py
+++ b/solution.py
@@ -521,16 +521,16 @@
     dv_turn(2)
     dv_total(0)
     dv_turn(3)
-
-    @pl.when(y == n - 1)
-    def _():
-        for xt in range(n):
-            fk_quarter(xt)
     dv_total(1)
     grad_query_half(k, dq_ref.at[k])
     dv_total(2)
     dv_total(3)
     fv_own().start()
+
+    @pl.when(y == n - 1)
+    def _():
+        for xt in range(n):
+            fk_quarter(xt)
     dk_final(0)
     for r, t_on, via in DV_VIA:
         dv_via(via, t_on)

time: 40.5 us -> 40.5 us (level)
  no operation moved by 1% of the time
where the time goes in v7:
time: 40.5 us; the launch traced here: 40.4 us
  Pallas kernels  39.6 us (98%)
  between operations  0.8 us (2%)
    pallas_call x1, Pallas kernels, per_device(): pl.pallas_call(functools.partial(kernel, tokens, heads, head), out_shape=...  38.3 us
    pallas_call x1, Pallas kernels, per_device(): pl.pallas_call(write_kernel, out_shape=shapes, in_specs=[vmem, vmem, vmem...  1.37 us

profile of v7, /device:TPU:97, one launch (start us, length us, event | category | flops | bytes accessed | tf_op | source)
XLA Modules:
  0.0 40.4 jit_solution(5784971751038799194)
XLA Ops:
  0.6 38.3 %shard_map.84 = (bf16[2,1024,256]{2,1,0:T(8,128)(2,1)S(1)}, bf16[2,1024,256]{2,1,0:T(8,128)(2,1)S(1)}, bf16[2,32,256]{2,1,0:T(8,128)(2,1)S(1)}, bf16[2,32,256]{2,1,0:T(8,128)(2,1)S(1)}) custom-call(s32[32]{0:T(128)} %pos_hbm.1, bf16[2,32,256]{2,1,0:T(8,128)(2,1)} %key_hbm.1, bf16[2,32,256]{2,1,0:T(8,128)(2,1)} %val_hbm.1, bf16[2,1024,256]{2,1,0:T(8,128)(2,1)} %bitcast.4, ...), custom_call_target="tpu_custom_call" | custom-call | tf_op jit(solution)/shard_map/pallas_call | solution.py:694
  38.9 1.4 %shard_map.85 = (bf16[2,1024,256]{2,1,0:T(8,128)(2,1)}, bf16[2,1024,256]{2,1,0:T(8,128)(2,1)}, bf16[2,32,256]{2,1,0:T(8,128)(2,1)}, bf16[2,32,256]{2,1,0:T(8,128)(2,1)}) custom-call(bf16[2,1024,256]{2,1,0:T(8,128)(2,1)S(1)} %get-tuple-element.12.a, bf16[2,1024,256]{2,1,0:T(8,128)(2,1)S(1)} %get-tuple-element.13.b, ...), custom_call_target="tpu_custom_call" | custom-call | tf_op jit(solution)/shard_map/pallas_call | solution.py:703
